TPU v7x, 32 devices: a 4x4x1 block of a 4x4x8 slice. The times are simulated.
32 devices in a mesh: data: 1 (over z), model: 32 (over y, x, core).
Axes of the slice: x: 4, y: 4, z: 1, core: 2. Of those that a mesh axis runs over, the one named last changes fastest.
The devices are a block of a 4x4x8 slice.
Arguments:
- hidden: bfloat16 [256, 4096], P(('data', 'model'))
- positions: int32 [256], P('data')
- attn_gain: bfloat16 [1, 4096], replicated
- mlp_gain: bfloat16 [1, 4096], replicated
- w_query: bfloat16 [1, 4096, 4096], P(None, None, 'model')
- w_key: bfloat16 [1, 4096, 4096], P(None, None, 'model')
- w_value: bfloat16 [1, 4096, 4096], P(None, None, 'model')
- w_out: bfloat16 [1, 4096, 4096], P(None, 'model')
- w_gate: bfloat16 [1, 4096, 11008], P(None, None, 'model')
- w_up: bfloat16 [1, 4096, 11008], P(None, None, 'model')
- w_down: bfloat16 [1, 11008, 4096], P(None, 'model')
- k_cache: bfloat16 [1, 256, 128, 32, 128], P(None, 'data', None, 'model')
- v_cache: bfloat16 [1, 256, 128, 32, 128], P(None, 'data', None, 'model')
Outputs:
- output 1: bfloat16 [256, 4096], P(('data', 'model'))
- output 2: bfloat16 [1, 256, 128, 32, 128], P(None, 'data', None, 'model')
- output 3: bfloat16 [1, 256, 128, 32, 128], P(None, 'data', None, 'model')
All inputs are finite; a program needn't handle non-finite values.
Results may differ from a plain program's by a relative error of at most 0.0157874.
Values are sent between devices in bfloat16 or wider.
A program may use at most 768 MiB of HBM per device.

v0:
```python
import jax
import jax.numpy as jnp
from jax import lax
from jax.sharding import PartitionSpec as P

NORM_EPS = 1e-5
ROPE_BASE = 10000.0


def rms_norm(row_vals, gain_vec):
    values_f = row_vals.astype(jnp.float32)
    inv_rms = lax.rsqrt(jnp.mean(values_f * values_f, axis=-1, keepdims=True) + NORM_EPS)
    return (values_f * inv_rms * gain_vec.astype(jnp.float32)).astype(jnp.bfloat16)


def rope_tables(positions, head_dim):
    half_dim = head_dim // 2
    inv_freq = ROPE_BASE ** (-2.0 * jnp.arange(half_dim, dtype=jnp.float32) / head_dim)
    angles = positions.astype(jnp.float32)[:, None] * inv_freq[None, :]
    return jnp.cos(angles), jnp.sin(angles)


def rope_rotate(head_vecs, cos_tab, sin_tab):
    half_dim = head_vecs.shape[-1] // 2
    lead_shape = (cos_tab.shape[0],) + (1,) * (head_vecs.ndim - 2) + (half_dim,)
    cos_b = cos_tab.reshape(lead_shape)
    sin_b = sin_tab.reshape(lead_shape)
    front_half = head_vecs[..., :half_dim].astype(jnp.float32)
    back_half = head_vecs[..., half_dim:].astype(jnp.float32)
    rotated = jnp.concatenate([front_half * cos_b - back_half * sin_b, back_half * cos_b + front_half * sin_b], axis=-1)
    return rotated.astype(jnp.bfloat16)


def attend(queries, k_layer, v_layer, positions):
    head_dim = queries.shape[-1]
    scores = jnp.einsum('bgrd,bsgd->bgrs', queries, k_layer, preferred_element_type=jnp.float32) * (head_dim ** -0.5)
    allowed = jnp.arange(k_layer.shape[1])[None, :] <= positions[:, None]
    scores = jnp.where(allowed[:, None, None, :], scores, -1e30)
    attn_probs = jax.nn.softmax(scores, axis=-1).astype(jnp.bfloat16)
    mixed_out = jnp.einsum('bgrs,bsgd->bgrd', attn_probs, v_layer, preferred_element_type=jnp.float32)
    return mixed_out.astype(jnp.bfloat16).reshape(queries.shape[0], -1)


def solution(mesh):
    row_spec = P(('data', 'model'), None)
    cache_spec = P(None, 'data', None, 'model', None)
    col_spec = P(None, None, 'model')
    inner_spec = P(None, 'model', None)
    in_specs = (row_spec, P('data'), P(), P(), col_spec, col_spec, col_spec, inner_spec, col_spec, col_spec, inner_spec, cache_spec, cache_spec)
    out_specs = (row_spec, cache_spec, cache_spec)

    def device_step(hidden, positions, attn_gain, mlp_gain, w_query, w_key, w_value, w_out, w_gate, w_up, w_down, k_cache, v_cache):
        n_layers = w_query.shape[0]
        n_tokens = positions.shape[0]
        local_kv = k_cache.shape[3]
        head_dim = k_cache.shape[4]
        group_size = w_query.shape[2] // (local_kv * head_dim)
        row_ids = jnp.arange(n_tokens)
        cos_tab, sin_tab = rope_tables(positions, head_dim)
        for layer_idx in range(n_layers):
            normed = rms_norm(hidden, attn_gain[layer_idx])
            gathered = lax.all_gather(normed, 'model', axis=0, tiled=True)
            queries = jnp.dot(gathered, w_query[layer_idx], preferred_element_type=jnp.float32).astype(jnp.bfloat16)
            keys_new = jnp.dot(gathered, w_key[layer_idx], preferred_element_type=jnp.float32).astype(jnp.bfloat16)
            values_new = jnp.dot(gathered, w_value[layer_idx], preferred_element_type=jnp.float32).astype(jnp.bfloat16)
            queries = rope_rotate(queries.reshape(n_tokens, local_kv, group_size, head_dim), cos_tab, sin_tab)
            keys_new = rope_rotate(keys_new.reshape(n_tokens, local_kv, head_dim), cos_tab, sin_tab)
            values_new = values_new.reshape(n_tokens, local_kv, head_dim)
            k_cache = k_cache.at[layer_idx, row_ids, positions].set(keys_new)
            v_cache = v_cache.at[layer_idx, row_ids, positions].set(values_new)
            attn_rows = attend(queries, k_cache[layer_idx], v_cache[layer_idx], positions)
            partial = jnp.dot(attn_rows, w_out[layer_idx], preferred_element_type=jnp.float32).astype(jnp.bfloat16)
            summed = lax.psum_scatter(partial, 'model', scatter_dimension=0, tiled=True)
            hidden = (hidden.astype(jnp.float32) + summed.astype(jnp.float32)).astype(jnp.bfloat16)
            normed = rms_norm(hidden, mlp_gain[layer_idx])
            gathered = lax.all_gather(normed, 'model', axis=0, tiled=True)
            gate_proj = jnp.dot(gathered, w_gate[layer_idx], preferred_element_type=jnp.float32)
            up_proj = jnp.dot(gathered, w_up[layer_idx], preferred_element_type=jnp.float32)
            mlp_act = (jax.nn.silu(gate_proj) * up_proj).astype(jnp.bfloat16)
            partial = jnp.dot(mlp_act, w_down[layer_idx], preferred_element_type=jnp.float32).astype(jnp.bfloat16)
            summed = lax.psum_scatter(partial, 'model', scatter_dimension=0, tiled=True)
            hidden = (hidden.astype(jnp.float32) + summed.astype(jnp.float32)).astype(jnp.bfloat16)
        return hidden, k_cache, v_cache

    return jax.shard_map(device_step, mesh=mesh, in_specs=in_specs, out_specs=out_specs, check_vma=False)
```

profile of v0, /device:TPU:97, one launch (start us, length us, event | category | flops | bytes accessed | tf_op | source)
XLA Modules:
  0.0 349.1 jit_solution(9453156155186219779)
XLA Ops:
  7.3 10.7 %copy.30 = bf16[1,256,128,1,128]{4,2,3,1,0:T(8,128)(2,1)} copy(bf16[1,256,128,1,128]{4,2,3,1,0:T(8,128)(2,1)} %param.24) | data formatting | bytes 16777216
  17.9 10.5 %copy.31 = bf16[1,256,128,1,128]{4,2,3,1,0:T(8,128)(2,1)} copy(bf16[1,256,128,1,128]{4,2,3,1,0:T(8,128)(2,1)} %param.25) | data formatting | bytes 16777216
  28.7 0.7 fusion.27
  29.5 0.2 reduce-scatter.3.cloned.1.call-start
  29.8 42.4 %all-gather.3.cloned.1.call-done = bf16[256,4096]{1,0:T(8,128)(2,1)} async-done(((bf16[8,4096]{1,0:T(8,128)(2,1)}), bf16[256,4096]{1,0:T(8,128)(2,1)}) %all-gather.3.cloned.1.call-update) | async-done | bytes 2097168 | tf_op jit(solution)/shard_map/all_gather | solution.py:62
  72.2 2.7 fusion.12
  74.9 0.3 fusion.46
  75.3 2.7 fusion.11
  78.0 0.3 fusion.56
  78.5 27.3 %scatter_fusion = bf16[256,128,128]{2,1,0:T(8,128)(2,1)} fusion(bf16[256,128,128]{2,1,0:T(8,128)(2,1)} %bitcast.67, s32[256]{0:T(256)S(1)} %bitcast.63, bf16[256,128]{1,0:T(8,128)(2,1)S(1)} %copy.18), kind=kCustom, calls=%fused_computation | custom fusion | bytes 198656 | tf_op jit(solution)/shard_map/scatter | solution.py:69
  105.8 7.9 %fusion.61 = f32[256,1,128]{2,1,0:T(1,128)S(1)} fusion(bf16[256,128,1]{1,2,0:T(2,128)(2,1)S(1)} %copy.20, bf16[256,128,128]{2,1,0:T(8,128)(2,1)} %scatter_fusion), kind=kOutput, calls=%fused_computation.85 | convolution fusion | flops 8388608 | bytes 8585216 | tf_op jit(solution)/shard_map/bgrd,bsgd->bgrs/dot_general | solution.py:36
  114.4 0.7 convolution_convert_fusion.2
  115.1 27.3 %scatter_fusion.1 = bf16[256,128,128]{2,1,0:T(8,128)(2,1)} fusion(bf16[256,128,128]{2,1,0:T(8,128)(2,1)} %bitcast.65, s32[256]{0:T(256)S(1)} %bitcast.64, bf16[256,128]{1,0:T(8,128)(2,1)S(1)} %convolution_convert_fusion.2), kind=kCustom, calls=%fused_computation.1 | custom fusion | bytes 198656 | tf_op jit(solution)/shard_map/scatter | solution.py:70
  142.4 5.7 %fusion.33 = f32[256,1,128]{2,1,0:T(1,128)S(1)} fusion(bf16[256,128,128]{2,1,0:T(8,128)(2,1)} %scatter_fusion.1, bf16[256,128,1]{1,0,2:T(8,128)(2,1)S(1)} %fusion.54), kind=kOutput, calls=%fused_computation.40 | convolution fusion | flops 8388608 | bytes 8585216 | tf_op jit(solution)/shard_map/bgrs,bsgd->bgrd/dot_general | solution.py:40
  148.2 2.0 convolution_convert_fusion.1
  150.4 68.6 %reduce-scatter.3.cloned.1.call-done = bf16[8,4096]{1,0:T(8,128)(2,1)} async-done(((bf16[256,4096]{1,0:T(8,128)(2,1)}), bf16[8,4096]{1,0:T(8,128)(2,1)}) %reduce-scatter.3.cloned.1.call-update) | async-done | bytes 65552 | tf_op jit(solution)/shard_map/reduce_scatter | solution.py:73
  219.0 1.0 fusion.29
  220.0 1.6 fusion.31
  221.6 0.3 reduce-scatter.5.cloned.1.call-start
  221.9 39.5 %all-gather.5.cloned.1.call-done = bf16[256,4096]{1,0:T(8,128)(2,1)} async-done(((bf16[8,4096]{1,0:T(8,128)(2,1)}), bf16[256,4096]{1,0:T(8,128)(2,1)}) %all-gather.5.cloned.1.call-update) | async-done | bytes 2097168 | tf_op jit(solution)/shard_map/all_gather | solution.py:76
  261.4 3.4 fusion.3
  264.8 7.4 %convolution_convert_fusion = bf16[256,4096]{1,0:T(8,128)(2,1)} fusion(bf16[1,344,4096]{2,1,0:T(8,128)(2,1)S(1)} %copy-done, bf16[256,4096]{1,0:T(8,128)(2,1)} %all-gather.5.cloned.1.call-done, bf16[1,4096,344]{1,2,0:T(8,128)(2,1)} %param.22, f32[256,344]{0,1:T(8,128)S(1)} %fusion.3), kind=kOutput, calls=%fused_computation.2 | convolution fusion | flops 1444417536 | bytes 10182656 | tf_op jit(solution)/shard_map/dot_general | solution.py:80
  272.3 68.7 %reduce-scatter.5.cloned.1.call-done = bf16[8,4096]{1,0:T(8,128)(2,1)} async-done(((bf16[256,4096]{1,0:T(8,128)(2,1)}), bf16[8,4096]{1,0:T(8,128)(2,1)}) %reduce-scatter.5.cloned.1.call-update) | async-done | bytes 65552 | tf_op jit(solution)/shard_map/reduce_scatter | solution.py:81
  341.0 1.5 fusion.32
  (39 shorter events, 1.5 us)
Async XLA Ops:
  7.2 257.6 %copy-start = (bf16[1,344,4096]{2,1,0:T(8,128)(2,1)S(1)}, bf16[1,344,4096]{2,1,0:T(8,128)(2,1)}, u32[]{:S(2)}) copy-start(bf16[1,344,4096]{2,1,0:T(8,128)(2,1)} %param.23) | copy-start | bytes 8454148
  7.2 65.0 %all-gather.3.cloned.1.call-start = ((), (), s32[]{:S(2)}) async-start(), calls=%async_computation.2 | async-start | bytes 2162688 | tf_op jit(solution)/shard_map/all_gather | solution.py:62
  17.9 10.6 %copy-start.7 = (bf16[1,4096]{1,0:T(2,128)(2,1)S(1)}, bf16[1,4096]{1,0:T(2,128)(2,1)}, u32[]{:S(2)}) copy-start(bf16[1,4096]{1,0:T(2,128)(2,1)} %param.15) | copy-start | bytes 24580
  17.9 10.6 %copy-start.2 = (bf16[8,4096]{1,0:T(8,128)(2,1)S(1)}, bf16[8,4096]{1,0:T(8,128)(2,1)}, u32[]{:S(2)}) copy-start(bf16[8,4096]{1,0:T(8,128)(2,1)} %param.13) | copy-start | bytes 196612
  17.9 11.8 %copy-start.6 = (s32[256]{0:T(256)S(1)}, s32[256]{0:T(256)}, u32[]{:S(2)}) copy-start(s32[256]{0:T(256)} %param.14) | copy-start | bytes 3076
  29.5 189.5 %reduce-scatter.3.cloned.1.call-start = ((), (), s32[]{:S(2)}) async-start(), calls=%async_computation.3 | async-start | bytes 2162688 | tf_op jit(solution)/shard_map/reduce_scatter | solution.py:73
  105.8 8.6 %copy-start.1 = (bf16[256,4096]{1,0:T(8,128)(2,1)S(1)}, bf16[256,4096]{1,0:T(8,128)(2,1)}, u32[]{:S(2)}) copy-start(bf16[256,4096]{1,0:T(8,128)(2,1)} %all-gather.3.cloned.1.call-done) | copy-start | bytes 6291460
  105.8 8.6 %copy-start.3 = (bf16[1,4096,128]{2,1,0:T(8,128)(2,1)S(1)}, bf16[1,4096,128]{2,1,0:T(8,128)(2,1)}, u32[]{:S(2)}) copy-start(bf16[1,4096,128]{2,1,0:T(8,128)(2,1)} %param.19) | copy-start | bytes 3145732
  142.4 5.7 %copy-start.4 = (bf16[1,128,4096]{2,1,0:T(8,128)(2,1)S(1)}, bf16[1,128,4096]{2,1,0:T(8,128)(2,1)}, u32[]{:S(2)}) copy-start(bf16[1,128,4096]{2,1,0:T(8,128)(2,1)} %param.20) | copy-start | bytes 3145732
  148.2 2.2 copy-start.8
  150.3 111.1 %all-gather.5.cloned.1.call-start = ((), (), s32[]{:S(2)}) async-start(), calls=%async_computation.4 | async-start | bytes 2162688 | tf_op jit(solution)/shard_map/all_gather | solution.py:76
  221.6 119.4 %reduce-scatter.5.cloned.1.call-start = ((), (), s32[]{:S(2)}) async-start(), calls=%async_computation.5 | async-start | bytes 2162688 | tf_op jit(solution)/shard_map/reduce_scatter | solution.py:81
  264.8 76.2 %copy-start.5 = (bf16[8,4096]{1,0:T(8,128)(2,1)S(1)}, bf16[8,4096]{1,0:T(8,128)(2,1)}, u32[]{:S(2)}) copy-start(bf16[8,4096]{1,0:T(8,128)(2,1)} %reduce-scatter.3.cloned.1.call-done) | copy-start | bytes 196612
Sparse Core Ops, SparseCore 0:
  29.6 42.5 all-gather.2
  150.4 68.4 reduce-scatter.2
  221.7 39.6 all-gather.4
  272.5 68.4 reduce-scatter.4
where the time goes:
time: 351 us; the launch traced here: 349 us
  waiting for transfers between devices  219 us (62%)
  local copies, waits for them, and re-layouts  76.1 us (22%)
  matrix products  32.6 us (9%)
  between operations  14 us (4%)
  other arithmetic  6.27 us (2%)
    reduce_scatter x2, waiting for transfers between devices, device_step(): summed = lax.psum_scatter(partial, 'model', scatter_dimension=0, tiled=True)  137 us
    all_gather x2, waiting for transfers between devices, device_step(): gathered = lax.all_gather(normed, 'model', axis=0, tiled=True)  82 us
    scatter x1, local copies, waits for them, and re-layouts, device_step(): k_cache = k_cache.at[layer_idx, row_ids, positions].set(keys_new)  27.3 us
    scatter x1, local copies, waits for them, and re-layouts, device_step(): v_cache = v_cache.at[layer_idx, row_ids, positions].set(values_new)  27.3 us
    unnamed x20, local copies, waits for them, and re-layouts  21.2 us
    dot_general x1, matrix products, attend(): jnp.einsum('bgrd,bsgd->bgrs', queries, k_layer, preferred_element_type=jn...  7.93 us
    dot_general x1, matrix products, device_step(): jnp.dot(mlp_act, w_down[layer_idx], preferred_element_type=jnp.float32)  7.45 us
  transfers between devices with their start and end apart: 4, of which 4 were waited for; matrix products, arithmetic and copies ran while one was open for 0% of the time, Pallas kernels for 0%

commit v1 on v0

v1 whole, which is shorter than its diff:
```python
import functools
import math

import jax
import jax.numpy as jnp
import numpy as np
from jax import lax
from jax.experimental import pallas as pl
from jax.experimental.pallas import tpu as pltpu
from jax.sharding import PartitionSpec as P

NORM_EPS = 1e-5
ROPE_BASE = 10000.0
CORES = 2
BF16 = jnp.bfloat16
F32 = jnp.float32


class Place:
    def __init__(self, side):
        me = lax.axis_index('model')
        self.side = side
        self.core = lax.rem(me, CORES)
        chip = me // CORES
        self.coord = (chip // side, lax.rem(chip, side))
        self.partner = self.device(self.coord, 1 - self.core)

    def device(self, coord, core):
        return {'model': (coord[0] * self.side + coord[1]) * CORES + core}

    def shift(self, axis, by):
        moved = list(self.coord)
        moved[axis] = lax.rem(moved[axis] + (by + self.side), self.side)
        return tuple(moved)

    def offset(self, first, by_first, by_second):
        moved = list(self.coord)
        moved[first] = lax.rem(moved[first] + (by_first + self.side), self.side)
        moved[1 - first] = lax.rem(moved[1 - first] + (by_second + self.side), self.side)
        return tuple(moved)

    def neighbour(self, axis, by):
        return self.device(self.shift(axis, by), self.core)

    def barrier(self):
        sem = pltpu.get_barrier_semaphore()
        others = [self.neighbour(axis, by) for axis in (0, 1) for by in (1, -1)] + [self.partner]
        for other in others:
            pl.semaphore_signal(sem, inc=1, device_id=other, device_id_type=pl.DeviceIdType.MESH)
        pl.semaphore_wait(sem, len(others))


def remote(src, dst, send, recv, device):
    return pltpu.make_async_remote_copy(src_ref=src, dst_ref=dst, send_sem=send, recv_sem=recv,
                                        device_id=device, device_id_type=pl.DeviceIdType.MESH)


GATHER_COPIES = 72


def all_gather(place, buf, send, recv):
    width = buf.shape[-1]
    half = width // 2
    started = []

    class Half:
        def __init__(self, h):
            self.first = 1 - h
            self.base = h * half
            self.sem = h * (GATHER_COPIES // 2)
            self.fp, self.fm = place.neighbour(self.first, 1), place.neighbour(self.first, -1)
            self.sp, self.sm = place.neighbour(1 - self.first, 1), place.neighbour(1 - self.first, -1)

        def copy(self, idx, a, b, part, device, core=None):
            coord = place.offset(self.first, a, b)
            lo = self.base + (half // 2 if part == 'hi' else 0)
            size = half if part == 'all' else half // 2
            ref = buf.at[coord[0], coord[1], place.core if core is None else core, :, pl.ds(lo, size)]
            return remote(ref, ref, send.at[self.sem + idx], recv.at[self.sem + idx], device)

        def start(self, *args):
            copy = self.copy(*args)
            copy.start()
            started.append(copy)

        def first_send(self):
            self.start(0, 0, 0, 'all', self.fp)
            self.start(1, 0, 0, 'all', self.fm)

        def first_take(self):
            self.copy(0, -1, 0, 'all', self.fp).wait_recv()
            self.start(2, -1, 0, 'lo', self.fp)
            self.copy(1, 1, 0, 'all', self.fm).wait_recv()
            self.start(3, 1, 0, 'hi', self.fm)

        def first_far(self):
            self.copy(2, -2, 0, 'lo', self.fp).wait_recv()
            self.copy(3, 2, 0, 'hi', self.fm).wait_recv()

        def slot(self, a):
            return 4 + 4 * (a + 1)

        def second_send(self, a):
            self.start(self.slot(a), a, 0, 'all', self.sp)
            self.start(self.slot(a) + 1, a, 0, 'all', self.sm)

        def second_take(self, a):
            self.copy(self.slot(a), a, -1, 'all', self.sp).wait_recv()
            self.start(self.slot(a) + 2, a, -1, 'lo', self.sp)
            self.copy(self.slot(a) + 1, a, 1, 'all', self.sm).wait_recv()
            self.start(self.slot(a) + 3, a, 1, 'hi', self.sm)
            self.twin(a, -1)
            self.twin(a, 1)

        def second_far(self, a):
            self.copy(self.slot(a) + 2, a, -2, 'lo', self.sp).wait_recv()
            self.copy(self.slot(a) + 3, a, 2, 'hi', self.sm).wait_recv()
            self.twin(a, 2)

        def twin_slot(self, a, b):
            return 20 + 4 * (a + 1) + (b + 1)

        def twin(self, a, b):
            self.start(self.twin_slot(a, b), a, b, 'all', place.partner)

        def twin_take(self, a, b):
            self.copy(self.twin_slot(a, b), a, b, 'all', place.partner, 1 - place.core).wait_recv()

    halves = (Half(0), Half(1))
    for h in halves:
        h.first_send()
    for h in halves:
        h.second_send(0)
        h.twin(0, 0)
    for h in halves:
        h.first_take()
        h.second_send(-1)
        h.second_send(1)
        h.twin(-1, 0)
        h.twin(1, 0)
    for h in halves:
        h.second_take(0)
    for h in halves:
        h.first_far()
        h.second_send(2)
        h.twin(2, 0)
    for h in halves:
        h.second_take(-1)
        h.second_take(1)
    for h in halves:
        h.second_far(0)
    for h in halves:
        h.second_take(2)
    for a in (-1, 1, 2):
        for h in halves:
            h.second_far(a)
    for h in halves:
        for a in (0, -1, 1, 2):
            for b in (0, -1, 1, 2):
                h.twin_take(a, b)
    return started


CHUNKS = 4
SCATTER_COPIES = 9 * CHUNKS


def scatter_scratch(side, rows, width):
    cw = width // CHUNKS
    return [
        pltpu.VMEM((side, side, CORES, rows, width), BF16),
        pltpu.VMEM((CHUNKS, side, side, rows, cw), BF16),
        pltpu.VMEM((CHUNKS, side, side, rows, cw), BF16),
        pltpu.VMEM((CHUNKS, 2, side, rows, cw // 2), BF16),
        pltpu.VMEM((CHUNKS, 2, side, rows, cw), BF16),
        pltpu.VMEM((CHUNKS, side, rows, cw), BF16),
        pltpu.VMEM((CHUNKS, 2, rows, cw // 2), BF16),
        pltpu.VMEM((CHUNKS, 2, rows, cw), BF16),
        pltpu.SemaphoreType.DMA((SCATTER_COPIES,)),
        pltpu.SemaphoreType.DMA((SCATTER_COPIES,)),
    ]


def reduce_scatter(place, compute, bufs, done):
    part, twin, total, land1, land2, mid, land3, land4, send, recv = bufs
    side, rows, width = part.shape[0], part.shape[3], part.shape[4]
    cw = width // CHUNKS
    hw = cw // 2
    started = []

    class Chunk:
        def __init__(self, i):
            self.i = i
            half = i % 2
            self.first = half
            self.base = (half * (CHUNKS // 2) + i // 2) * cw
            self.sem = i * 9
            f, s = self.first, 1 - self.first
            self.fp, self.fm = place.neighbour(f, 1), place.neighbour(f, -1)
            self.sp, self.sm = place.neighbour(s, 1), place.neighbour(s, -1)

        def at(self, axis, by):
            return place.shift(axis, by)[axis]

        def plane(self, ref, by):
            idx = self.at(self.first, by)
            return ref.at[self.i, idx] if self.first == 0 else ref.at[self.i, :, idx]

        def start(self, k, src, dst, device):
            copy = remote(src, dst, send.at[self.sem + k], recv.at[self.sem + k], device)
            copy.start()
            started.append(copy)

        def take(self, k, dst, device):
            remote(dst, dst, send.at[self.sem + k], recv.at[self.sem + k], device).wait_recv()

        def compute(self):
            value = compute(self.base, cw)
            part[:, :, :, :, pl.ds(self.base, cw)] = value.reshape(side, side, CORES, rows, cw).astype(BF16)
            self.start(0, part.at[:, :, 1 - place.core, :, pl.ds(self.base, cw)], twin.at[self.i], place.partner)

        def stage1(self):
            self.take(0, twin.at[self.i], place.partner)
            own = part[:, :, place.core, :, pl.ds(self.base, cw)].astype(F32)
            total[self.i] = (own + twin[self.i].astype(F32)).astype(BF16)
            far = self.plane(total, 2)
            self.start(1, far.at[:, :, pl.ds(0, hw)], land1.at[self.i, 0], self.fp)
            self.start(2, far.at[:, :, pl.ds(hw, hw)], land1.at[self.i, 1], self.fm)

        def stage2(self):
            for k, by, dev in ((0, 1, self.fp), (1, -1, self.fm)):
                self.take(1 + k, land1.at[self.i, k], dev)
                ref = self.plane(total, by)
                cols = (slice(None), slice(None), pl.ds(k * hw, hw))
                ref[cols] = (ref[cols].astype(F32) + land1[self.i, k].astype(F32)).astype(BF16)
                self.start(3 + k, ref, land2.at[self.i, k], dev)

        def stage3(self):
            self.take(3, land2.at[self.i, 0], self.fp)
            self.take(4, land2.at[self.i, 1], self.fm)
            own = self.plane(total, 0)[...].astype(F32)
            mid[self.i] = (own + land2[self.i, 0].astype(F32) + land2[self.i, 1].astype(F32)).astype(BF16)
            far = mid.at[self.i, self.at(1 - self.first, 2)]
            self.start(5, far.at[:, pl.ds(0, hw)], land3.at[self.i, 0], self.sp)
            self.start(6, far.at[:, pl.ds(hw, hw)], land3.at[self.i, 1], self.sm)

        def stage4(self):
            for k, by, dev in ((0, 1, self.sp), (1, -1, self.sm)):
                self.take(5 + k, land3.at[self.i, k], dev)
                ref = mid.at[self.i, self.at(1 - self.first, by)]
                cols = (slice(None), pl.ds(k * hw, hw))
                ref[cols] = (ref[cols].astype(F32) + land3[self.i, k].astype(F32)).astype(BF16)
                self.start(7 + k, ref, land4.at[self.i, k], dev)

        def stage5(self):
            self.take(7, land4.at[self.i, 0], self.sp)
            self.take(8, land4.at[self.i, 1], self.sm)
            own = mid[self.i, self.at(1 - self.first, 0)].astype(F32)
            done(self.base, own + land4[self.i, 0].astype(F32) + land4[self.i, 1].astype(F32))

    chunks = [Chunk(i) for i in range(CHUNKS)]
    for stage in ('compute', 'stage1', 'stage2', 'stage3', 'stage4', 'stage5'):
        for chunk in chunks:
            getattr(chunk, stage)()
    return started


def norm_rows(values, gain):
    inv = lax.rsqrt(jnp.mean(values * values, axis=-1, keepdims=True) + NORM_EPS)
    return (values * inv * gain).astype(BF16)


def flat_rows(buf):
    width = buf.shape[-1]
    return buf[...].astype(F32).reshape(-1, width).astype(BF16)


def qkv_kernel(side, x_ref, gain_ref, pos_ref, freq_ref, wq_hbm, wk_hbm, wv_hbm, q_ref, k_ref, v_ref,
               w_buf, gath, w_sem, send, recv):
    place = Place(side)
    head = q_ref.shape[1]
    loads = []
    for i, w in enumerate((wq_hbm, wk_hbm, wv_hbm)):
        loads.append(pltpu.make_async_copy(w, w_buf.at[:, pl.ds(i * head, head)], w_sem.at[i]))
        loads[-1].start()
    own = norm_rows(x_ref[...].astype(F32), gain_ref[...].astype(F32))
    gath[place.coord[0], place.coord[1], place.core] = own
    place.barrier()
    sent = all_gather(place, gath, send, recv)
    for load in loads:
        load.wait()
    rows = flat_rows(gath)
    out = jnp.dot(rows, w_buf[...], preferred_element_type=F32).astype(BF16)
    angle = pos_ref[...].astype(F32) * freq_ref[...]
    cos, sin = jnp.cos(angle), jnp.sin(angle)
    lane = lax.broadcasted_iota(jnp.int32, sin.shape, 1)
    sin = jnp.where(lane < head // 2, -sin, sin)

    def rotate(vec):
        vec = vec.astype(F32)
        return (vec * cos + pltpu.roll(vec, head // 2, 1) * sin).astype(BF16)

    q_ref[...] = rotate(out[:, :head])
    k_ref[...] = rotate(out[:, head:2 * head])
    v_ref[...] = out[:, 2 * head:]
    for copy in sent:
        copy.wait_send()


def qkv_call(side, hidden, gain, pos_col, freq, wq, wk, wv):
    rows, width = hidden.shape
    tokens = pos_col.shape[0]
    head = wq.shape[1]
    vmem, hbm = pl.BlockSpec(memory_space=pltpu.VMEM), pl.BlockSpec(memory_space=pl.ANY)
    shape = jax.ShapeDtypeStruct((tokens, head), BF16)
    return pl.pallas_call(
        functools.partial(qkv_kernel, side),
        out_shape=(shape, shape, shape),
        in_specs=[vmem, vmem, vmem, vmem, hbm, hbm, hbm],
        out_specs=(vmem, vmem, vmem),
        scratch_shapes=[
            pltpu.VMEM((width, 3 * head), BF16),
            pltpu.VMEM((side, side, CORES, rows, width), BF16),
            pltpu.SemaphoreType.DMA((3,)),
            pltpu.SemaphoreType.DMA((GATHER_COPIES,)),
            pltpu.SemaphoreType.DMA((GATHER_COPIES,)),
        ],
        compiler_params=pltpu.CompilerParams(collective_id=0, has_side_effects=True, vmem_limit_bytes=24 << 20),
        cost_estimate=pl.CostEstimate(flops=20_000_000_000, bytes_accessed=8 << 20, transcendentals=0),
        name='gather_qkv',
    )(hidden, gain, pos_col, freq, wq, wk, wv)


TOKEN_BLOCK = 16


def attend_kernel(pos_smem, pos_ref, q_ref, k_ref, v_ref, kc_hbm, vc_hbm, o_ref, ko_hbm, vo_hbm,
                  kbuf, vbuf, in_sem, out_sem):
    tokens, length, head = kbuf.shape
    blocks = tokens // TOKEN_BLOCK
    caches = ((kc_hbm, kbuf, ko_hbm), (vc_hbm, vbuf, vo_hbm))

    def load(b, j):
        src, buf, _ = caches[j]
        at = pl.ds(b * TOKEN_BLOCK, TOKEN_BLOCK)
        return pltpu.make_async_copy(src.at[at], buf.at[at], in_sem.at[j, b])

    def store(b, j):
        _, buf, dst = caches[j]
        at = pl.ds(b * TOKEN_BLOCK, TOKEN_BLOCK)
        return pltpu.make_async_copy(buf.at[at], dst.at[at], out_sem.at[j, b])

    for b in range(blocks):
        load(b, 0).start()
        load(b, 1).start()
    group = 16
    row = lax.broadcasted_iota(jnp.int32, (group, head), 0)
    lane = lax.broadcasted_iota(jnp.int32, (TOKEN_BLOCK, length), 1)
    pick = lax.broadcasted_iota(jnp.int32, (TOKEN_BLOCK, head), 0)

    def block(b, carry):
        base = pl.multiple_of(b * TOKEN_BLOCK, TOKEN_BLOCK)
        at = pl.ds(base, TOKEN_BLOCK)
        load(b, 0).wait()
        load(b, 1).wait()
        news = (k_ref[at, :].astype(F32), v_ref[at, :].astype(F32))
        for t in range(TOKEN_BLOCK):
            p = pos_smem[base + t]
            lo = pl.multiple_of((p // group) * group, group)
            for j, buf in ((0, kbuf), (1, vbuf)):
                old = buf[base + t, pl.ds(lo, group), :].astype(F32)
                new = jnp.broadcast_to(news[j][t:t + 1, :], (group, head))
                buf[base + t, pl.ds(lo, group), :] = jnp.where(row == p - lo, new, old).astype(BF16)
        store(b, 0).start()
        store(b, 1).start()
        q = q_ref[at, :].astype(F32)
        scores = jnp.zeros((TOKEN_BLOCK, length), F32)
        for t in range(0, TOKEN_BLOCK, 2):
            pair = jnp.concatenate([kbuf[base + t], kbuf[base + t + 1]], axis=1)
            left = jnp.where(pick == t, q, 0.0)
            right = jnp.where(pick == t + 1, q, 0.0)
            lhs = jnp.concatenate([left, right], axis=1).astype(BF16)
            scores += lax.dot_general(lhs, pair, (((1,), (1,)), ((), ())), preferred_element_type=F32)
        scores = scores * (head ** -0.5)
        scores = jnp.where(lane <= pos_ref[at, :], scores, -1e30)
        top = jnp.max(scores, axis=-1, keepdims=True)
        probs = jnp.exp(scores - top)
        probs = (probs / jnp.sum(probs, axis=-1, keepdims=True)).astype(BF16)
        mixed = jnp.zeros((TOKEN_BLOCK, head), F32)
        for t in range(0, TOKEN_BLOCK, 2):
            pair = jnp.concatenate([vbuf[base + t], vbuf[base + t + 1]], axis=1)
            both = jnp.dot(probs, pair, preferred_element_type=F32)
            mixed = jnp.where(pick == t, both[:, :head], mixed)
            mixed = jnp.where(pick == t + 1, both[:, head:], mixed)
        o_ref[at, :] = mixed.astype(BF16)
        return carry

    lax.fori_loop(0, blocks, block, 0)
    for b in range(blocks):
        store(b, 0).wait()
        store(b, 1).wait()


def attend_call(positions, pos_col, q, k, v, kc, vc):
    tokens, length, head = kc.shape
    blocks = tokens // TOKEN_BLOCK
    vmem, hbm = pl.BlockSpec(memory_space=pltpu.VMEM), pl.BlockSpec(memory_space=pl.ANY)
    cache = jax.ShapeDtypeStruct(kc.shape, BF16)
    return pl.pallas_call(
        attend_kernel,
        out_shape=(jax.ShapeDtypeStruct(q.shape, BF16), cache, cache),
        in_specs=[pl.BlockSpec(memory_space=pltpu.SMEM), vmem, vmem, vmem, vmem, hbm, hbm],
        out_specs=(vmem, hbm, hbm),
        scratch_shapes=[
            pltpu.VMEM(kc.shape, BF16),
            pltpu.VMEM(kc.shape, BF16),
            pltpu.SemaphoreType.DMA((2, blocks)),
            pltpu.SemaphoreType.DMA((2, blocks)),
        ],
        compiler_params=pltpu.CompilerParams(vmem_limit_bytes=60 << 20),
        cost_estimate=pl.CostEstimate(flops=20_000_000_000, bytes_accessed=32 << 20, transcendentals=0),
        name='attend',
    )(positions, pos_col, q, k, v, kc, vc)


def block_kernel(side, x_ref, gain_ref, o_ref, wo_hbm, wg_hbm, wu_hbm, wd_hbm, out_ref,
                 wo, wg, wu, wd, mid_rows, act, gath, w_sem, g_send, g_recv, *bufs):
    place = Place(side)
    count = len(bufs) // 2
    loads = []
    for i, (src, dst) in enumerate(((wo_hbm, wo), (wg_hbm, wg), (wu_hbm, wu), (wd_hbm, wd))):
        loads.append(pltpu.make_async_copy(src, dst, w_sem.at[i]))
        loads[-1].start()
    place.barrier()
    loads[0].wait()

    def out_proj(base, size):
        return jnp.dot(o_ref[...], wo[:, pl.ds(base, size)], preferred_element_type=F32)

    def out_done(base, value):
        cols = pl.ds(base, value.shape[1])
        mid_rows[:, cols] = (x_ref[:, cols].astype(F32) + value).astype(BF16).astype(F32)

    sent = reduce_scatter(place, out_proj, bufs[:count], out_done)
    gath[place.coord[0], place.coord[1], place.core] = norm_rows(mid_rows[...], gain_ref[...].astype(F32))
    sent += all_gather(place, gath, g_send, g_recv)
    loads[1].wait()
    loads[2].wait()
    rows = flat_rows(gath)
    nt = (((1,), (1,)), ((), ()))
    gate = lax.dot_general(rows, wg[...], nt, preferred_element_type=F32)
    up = lax.dot_general(rows, wu[...], nt, preferred_element_type=F32)
    act[...] = (gate * jax.nn.sigmoid(gate) * up).astype(BF16)
    loads[3].wait()

    def down_proj(base, size):
        return jnp.dot(act[...], wd[:, pl.ds(base, size)], preferred_element_type=F32)

    def down_done(base, value):
        cols = pl.ds(base, value.shape[1])
        out_ref[:, cols] = (mid_rows[:, cols] + value).astype(BF16)

    sent += reduce_scatter(place, down_proj, bufs[count:], down_done)
    for copy in sent:
        copy.wait_send()


def block_call(side, hidden, gain, attn, wo, wg, wu, wd):
    rows, width = hidden.shape
    tokens = attn.shape[0]
    vmem, hbm = pl.BlockSpec(memory_space=pltpu.VMEM), pl.BlockSpec(memory_space=pl.ANY)
    return pl.pallas_call(
        functools.partial(block_kernel, side),
        out_shape=jax.ShapeDtypeStruct(hidden.shape, BF16),
        in_specs=[vmem, vmem, vmem, hbm, hbm, hbm, hbm],
        out_specs=vmem,
        scratch_shapes=[
            pltpu.VMEM(wo.shape, BF16),
            pltpu.VMEM(wg.shape, BF16),
            pltpu.VMEM(wu.shape, BF16),
            pltpu.VMEM(wd.shape, BF16),
            pltpu.VMEM((rows, width), F32),
            pltpu.VMEM((tokens, wg.shape[0]), BF16),
            pltpu.VMEM((side, side, CORES, rows, width), BF16),
            pltpu.SemaphoreType.DMA((4,)),
            pltpu.SemaphoreType.DMA((GATHER_COPIES,)),
            pltpu.SemaphoreType.DMA((GATHER_COPIES,)),
        ] + scatter_scratch(side, rows, width) * 2,
        compiler_params=pltpu.CompilerParams(collective_id=1, has_side_effects=True, vmem_limit_bytes=60 << 20),
        cost_estimate=pl.CostEstimate(flops=60_000_000_000, bytes_accessed=16 << 20, transcendentals=0),
        name='project_mlp',
    )(hidden, gain, attn, wo, wg, wu, wd)


def solution(mesh):
    row_spec = P(('data', 'model'), None)
    cache_spec = P(None, 'data', None, 'model', None)
    col_spec = P(None, None, 'model')
    inner_spec = P(None, 'model', None)
    in_specs = (row_spec, P('data'), P(), P(), col_spec, col_spec, col_spec, inner_spec, col_spec, col_spec, inner_spec, cache_spec, cache_spec)
    out_specs = (row_spec, cache_spec, cache_spec)
    side = math.isqrt(mesh.shape['model'] // CORES)

    def device_step(hidden, positions, attn_gain, mlp_gain, w_query, w_key, w_value, w_out, w_gate, w_up, w_down, k_cache, v_cache):
        n_layers, n_tokens = w_query.shape[0], positions.shape[0]
        length, heads, head = k_cache.shape[2:]
        pos_col = positions.reshape(n_tokens, 1)
        freq = ROPE_BASE ** (-2.0 * np.arange(head // 2, dtype=np.float32) / np.float32(head))
        freq = jnp.asarray(np.concatenate([freq, freq])[None, :].astype(np.float32))
        k_out, v_out = [], []
        for i in range(n_layers):
            q, k, v = qkv_call(side, hidden, attn_gain[i:i + 1], pos_col, freq, w_query[i], w_key[i], w_value[i])
            shape = (n_tokens, length, head)
            attn, kc, vc = attend_call(positions, pos_col, q, k, v, k_cache[i].reshape(shape), v_cache[i].reshape(shape))
            k_out.append(kc.reshape(k_cache.shape[1:]))
            v_out.append(vc.reshape(v_cache.shape[1:]))
            hidden = block_call(side, hidden, mlp_gain[i:i + 1], attn, w_out[i], w_gate[i].T, w_up[i].T, w_down[i])
        return hidden, jnp.stack(k_out), jnp.stack(v_out)

    return jax.shard_map(device_step, mesh=mesh, in_specs=in_specs, out_specs=out_specs, check_vma=False)
```

time: 351 us -> 111 us (0.32)
  waiting for transfers between devices: 219 us -> 0 us
  Pallas kernels: 0 us -> 98.9 us
  local copies, waits for them, and re-layouts: 76.1 us -> 10 us
  matrix products: 32.6 us -> 0 us
  between operations: 14 us -> 0.69 us
  other arithmetic: 6.27 us -> 0 us
    reduce_scatter x2 -> x0, waiting for transfers between devices: 137 us -> none  [device_step(): summed = lax.psum_scatter(partial, 'model', scatter_dimension=0, tiled=True)]
    pallas_call x0 -> x3, Pallas kernels: none -> 98.9 us  [the longest x1 56.9 us: block_call(): pl.pallas_call(functools.partial(block_kernel, side), out_shape=jax.Shape...]
    all_gather x2 -> x0, waiting for transfers between devices: 82 us -> none  [device_step(): gathered = lax.all_gather(normed, 'model', axis=0, tiled=True)]
    scatter x2 -> x0, local copies, waits for them, and re-layouts: 54.7 us -> none  [the longest x1 27.3 us: device_step(): k_cache = k_cache.at[layer_idx, row_ids, positions].set(keys_new)]
    dot_general x8 -> x0, matrix products: 32.6 us -> none  [the longest x1 7.93 us: attend(): jnp.einsum('bgrd,bsgd->bgrs', queries, k_layer, preferred_element_type=jn...]
    unnamed x20 -> x21, local copies, waits for them, and re-layouts: 21.2 us -> 9.22 us
    convert_element_type x5 -> x0, other arithmetic: 3.95 us -> none  [the longest x2 2.28 us: rms_norm(): (values_f * inv_rms * gain_vec.astype(jnp.float32)).astype(jnp.bfloat16)]
  transfers between devices with their start and end apart: 4 -> 0, of which waited for: 4 -> 0; matrix products, arithmetic and copies ran while one was open for 0% -> 0% of each run, Pallas kernels for 0% -> 0%
where the time goes in v1:
time: 111 us; the launch traced here: 110 us
  Pallas kernels  98.9 us (89%)
  local copies, waits for them, and re-layouts  10 us (9%)
    pallas_call x1, Pallas kernels, block_call(): pl.pallas_call(functools.partial(block_kernel, side), out_shape=jax.Shape...  56.9 us
    pallas_call x1, Pallas kernels, qkv_call(): pl.pallas_call(functools.partial(qkv_kernel, side), out_shape=(shape, sha...  25.1 us
    pallas_call x1, Pallas kernels, attend_call(): pl.pallas_call(attend_kernel, out_shape=(jax.ShapeDtypeStruct(q.shape, BF...  16.9 us
    unnamed x21, local copies, waits for them, and re-layouts  9.22 us

profile of v1, /device:TPU:97, one launch (start us, length us, event | category | flops | bytes accessed | tf_op | source)
XLA Modules:
  0.0 109.6 jit_solution(451363399773669749)
XLA Ops:
  0.6 0.8 copy.20.pos_ref
  1.4 0.0 copy-start.1
  1.5 1.2 %copy-done.1 = bf16[1,4096,128]{2,1,0:T(8,128)(2,1)S(1)} copy-done((bf16[1,4096,128]{2,1,0:T(8,128)(2,1)S(1)}, bf16[1,4096,128]{2,1,0:T(8,128)(2,1)}, u32[]{:S(2)}) %copy-start.1) | copy-done | bytes 1048600
  2.7 0.0 copy-start.2
  2.7 1.2 %copy-done.2 = bf16[1,4096,128]{2,1,0:T(8,128)(2,1)S(1)} copy-done((bf16[1,4096,128]{2,1,0:T(8,128)(2,1)S(1)}, bf16[1,4096,128]{2,1,0:T(8,128)(2,1)}, u32[]{:S(2)}) %copy-start.2) | copy-done | bytes 1048600
  3.9 0.0 copy-start.3
  3.9 1.2 %copy-done.3 = bf16[1,4096,128]{2,1,0:T(8,128)(2,1)S(1)} copy-done((bf16[1,4096,128]{2,1,0:T(8,128)(2,1)S(1)}, bf16[1,4096,128]{2,1,0:T(8,128)(2,1)}, u32[]{:S(2)}) %copy-start.3) | copy-done | bytes 1048600
  5.1 0.0 copy-start.4
  5.1 0.8 copy-done.4
  6.0 0.0 copy-start.5
  6.0 0.7 copy-done.5
  6.7 0.0 copy-start.6
  6.7 0.7 copy-done.6
  7.3 0.0 copy-start
  7.3 25.1 %gather_qkv.1 = (bf16[256,128]{1,0:T(8,128)(2,1)S(1)}, bf16[256,128]{1,0:T(8,128)(2,1)S(1)}, bf16[256,128]{1,0:T(8,128)(2,1)S(1)}) custom-call(bf16[8,4096]{1,0:T(8,128)(2,1)S(1)} %copy-done.4, bf16[1,4096]{1,0:T(2,128)(2,1)S(1)} %copy-done.5, s32[256,1]{1,0:T(8,128)S(1)} %copy.20.pos_ref, f32[1,128]{1,0:T(1,128)S(1)} %copy-done.6, ...), custom_call_target="tpu_custom_call" | custom-call | flops 20000000000 | bytes 8388608 | tf_op jit(solution)/shard_map/gather_qkv/pallas_call | solution.py:316
  32.4 0.0 copy-done
  32.4 0.0 copy-start.7
  32.4 0.6 copy-done.7
  33.1 0.0 copy-start.8
  33.1 0.6 copy-done.8
  33.7 0.6 copy-done.9
  34.3 16.9 %attend.1 = (bf16[256,128]{1,0:T(8,128)(2,1)}, bf16[256,128,128]{2,1,0:T(8,128)(2,1)}, bf16[256,128,128]{2,1,0:T(8,128)(2,1)}) custom-call(s32[256]{0:T(256)} %pos_smem.1, s32[256,1]{1,0:T(8,128)} %copy-done, bf16[256,128]{1,0:T(8,128)(2,1)} %copy-done.7, bf16[256,128]{1,0:T(8,128)(2,1)} %copy-done.8, bf16[256,128]{1,0:T(8,128)(2,1)} %copy-done.9, ...), custom_call_target="tpu_custom_call" | custom-call | flops 20000000000 | bytes 33554432 | tf_op jit(solution)/shard_map/attend/pallas_call | solution.py:409
  51.2 56.9 %project_mlp.1 = bf16[8,4096]{1,0:T(8,128)(2,1)} custom-call(bf16[8,4096]{1,0:T(8,128)(2,1)} %x_ref.3, bf16[1,4096]{1,0:T(2,128)(2,1)} %gain_ref.3, bf16[256,128]{1,0:T(8,128)(2,1)} %get-tuple-element.12.o_ref, bf16[128,4096]{1,0:T(8,128)(2,1)} %bitcast.29, bf16[344,4096]{1,0:T(8,128)(2,1)} %bitcast.26, bf16[344,4096]{1,0:T(8,128)(2,1)} %bitcast.27, ...), custom_call_target="tpu_custom_call" | custom-call | flops 60000002048 | bytes 16777216 | tf_op jit(solution)/shard_map/project_mlp/pallas_call | solution.py:472
  108.1 1.5 %copy.24 = bf16[8,4096]{1,0:T(8,128)(2,1)} copy(bf16[8,4096]{1,0:T(8,128)(2,1)} %project_mlp.1) | data formatting | bytes 131072
  (1 shorter events, 0.0 us)
Async XLA Ops:
  1.4 1.2 %copy-start.1 = (bf16[1,4096,128]{2,1,0:T(8,128)(2,1)S(1)}, bf16[1,4096,128]{2,1,0:T(8,128)(2,1)}, u32[]{:S(2)}) copy-start(bf16[1,4096,128]{2,1,0:T(8,128)(2,1)} %param.18) | copy-start | bytes 3145732
  2.7 1.2 %copy-start.2 = (bf16[1,4096,128]{2,1,0:T(8,128)(2,1)S(1)}, bf16[1,4096,128]{2,1,0:T(8,128)(2,1)}, u32[]{:S(2)}) copy-start(bf16[1,4096,128]{2,1,0:T(8,128)(2,1)} %param.19) | copy-start | bytes 3145732
  3.9 1.2 %copy-start.3 = (bf16[1,4096,128]{2,1,0:T(8,128)(2,1)S(1)}, bf16[1,4096,128]{2,1,0:T(8,128)(2,1)}, u32[]{:S(2)}) copy-start(bf16[1,4096,128]{2,1,0:T(8,128)(2,1)} %param.20) | copy-start | bytes 3145732
  5.1 0.8 copy-start.4
  6.0 0.7 copy-start.5
  6.7 0.7 copy-start.6
  7.3 25.1 %copy-start = (s32[256,1]{1,0:T(8,128)}, s32[256,1]{1,0:T(8,128)S(1)}, u32[]{:S(2)}) copy-start(s32[256,1]{1,0:T(8,128)S(1)} %copy.20.pos_ref) | copy-start | bytes 3076
  32.4 0.6 copy-start.7
  33.1 0.6 copy-start.8
  33.7 0.6 copy-start.9

commit v2 on v1

--- a/solution.py
+++ b/solution.py
@@ -42,12 +42,14 @@
     def neighbour(self, axis, by):
         return self.device(self.shift(axis, by), self.core)
 
-    def barrier(self):
-        sem = pltpu.get_barrier_semaphore()
+    def barrier_signal(self):
         others = [self.neighbour(axis, by) for axis in (0, 1) for by in (1, -1)] + [self.partner]
         for other in others:
-            pl.semaphore_signal(sem, inc=1, device_id=other, device_id_type=pl.DeviceIdType.MESH)
-        pl.semaphore_wait(sem, len(others))
+            pl.semaphore_signal(pltpu.get_barrier_semaphore(), inc=1, device_id=other,
+                                device_id_type=pl.DeviceIdType.MESH)
+
+    def barrier_wait(self):
+        pl.semaphore_wait(pltpu.get_barrier_semaphore(), 5)
 
 
 def remote(src, dst, send, recv, device):
@@ -58,7 +60,7 @@
 GATHER_COPIES = 72
 
 
-def all_gather(place, buf, send, recv):
+def all_gather(place, buf, send, recv, idle=None):
     width = buf.shape[-1]
     half = width // 2
     started = []
@@ -132,6 +134,8 @@
     for h in halves:
         h.second_send(0)
         h.twin(0, 0)
+    if idle is not None:
+        idle()
     for h in halves:
         h.first_take()
         h.second_send(-1)
@@ -275,26 +279,39 @@
     return buf[...].astype(F32).reshape(-1, width).astype(BF16)
 
 
-def qkv_kernel(side, x_ref, gain_ref, pos_ref, freq_ref, wq_hbm, wk_hbm, wv_hbm, q_ref, k_ref, v_ref,
-               w_buf, gath, w_sem, send, recv):
+def qkv_kernel(side, x_hbm, gain_hbm, pos_hbm, freq_hbm, wq_hbm, wk_hbm, wv_hbm, kc_hbm, vc_hbm,
+               q_ref, k_ref, v_ref, kbuf, vbuf,
+               x_buf, gain_buf, pos_buf, freq_buf, w_buf, gath, s_sem, w_sem, send, recv):
     place = Place(side)
     head = q_ref.shape[1]
-    loads = []
-    for i, w in enumerate((wq_hbm, wk_hbm, wv_hbm)):
-        loads.append(pltpu.make_async_copy(w, w_buf.at[:, pl.ds(i * head, head)], w_sem.at[i]))
-        loads[-1].start()
-    own = norm_rows(x_ref[...].astype(F32), gain_ref[...].astype(F32))
+    small = [pltpu.make_async_copy(src, dst, s_sem.at[i]) for i, (src, dst) in enumerate(
+        ((x_hbm, x_buf), (gain_hbm, gain_buf), (pos_hbm, pos_buf), (freq_hbm, freq_buf)))]
+    large = [pltpu.make_async_copy(w, w_buf.at[:, pl.ds(i * head, head)], w_sem.at[i])
+             for i, w in enumerate((wq_hbm, wk_hbm, wv_hbm))]
+    caches = [pltpu.make_async_copy(kc_hbm, kbuf, w_sem.at[3]), pltpu.make_async_copy(vc_hbm, vbuf, w_sem.at[4])]
+    for copy in small + large:
+        copy.start()
+    place.barrier_signal()
+    for copy in small:
+        copy.wait()
+    own = norm_rows(x_buf[...].astype(F32), gain_buf[...].astype(F32))
     gath[place.coord[0], place.coord[1], place.core] = own
-    place.barrier()
-    sent = all_gather(place, gath, send, recv)
-    for load in loads:
-        load.wait()
-    rows = flat_rows(gath)
-    out = jnp.dot(rows, w_buf[...], preferred_element_type=F32).astype(BF16)
-    angle = pos_ref[...].astype(F32) * freq_ref[...]
+    place.barrier_wait()
+
+    def idle():
+        for copy in caches:
+            copy.start()
+
+    sent = all_gather(place, gath, send, recv, idle)
+    pos = jnp.broadcast_to(pos_buf[...].astype(F32), (head, pos_buf.shape[1])).T
+    angle = pos * freq_buf[...]
     cos, sin = jnp.cos(angle), jnp.sin(angle)
     lane = lax.broadcasted_iota(jnp.int32, sin.shape, 1)
     sin = jnp.where(lane < head // 2, -sin, sin)
+    for copy in large:
+        copy.wait()
+    rows = flat_rows(gath)
+    out = jnp.dot(rows, w_buf[...], preferred_element_type=F32).astype(BF16)
 
     def rotate(vec):
         vec = vec.astype(F32)
@@ -305,54 +322,61 @@
     v_ref[...] = out[:, 2 * head:]
     for copy in sent:
         copy.wait_send()
-
-
-def qkv_call(side, hidden, gain, pos_col, freq, wq, wk, wv):
+    for copy in caches:
+        copy.wait()
+
+
+def in_hbm(*arrays):
+    return [pltpu.with_memory_space_constraint(a, pltpu.HBM) for a in arrays]
+
+
+def in_vmem(*arrays):
+    return [pltpu.with_memory_space_constraint(a, pltpu.VMEM) for a in arrays]
+
+
+def qkv_call(side, hidden, gain, pos_row, freq, wq, wk, wv, kc, vc):
     rows, width = hidden.shape
-    tokens = pos_col.shape[0]
+    tokens = pos_row.shape[1]
     head = wq.shape[1]
-    vmem, hbm = pl.BlockSpec(memory_space=pltpu.VMEM), pl.BlockSpec(memory_space=pl.ANY)
-    shape = jax.ShapeDtypeStruct((tokens, head), BF16)
+    vmem, hbm = pl.BlockSpec(memory_space=pltpu.VMEM), pl.BlockSpec(memory_space=pltpu.HBM)
+    shape = pltpu.VMEM((tokens, head), BF16)
+    cache = pltpu.VMEM(kc.shape, BF16)
     return pl.pallas_call(
         functools.partial(qkv_kernel, side),
-        out_shape=(shape, shape, shape),
-        in_specs=[vmem, vmem, vmem, vmem, hbm, hbm, hbm],
-        out_specs=(vmem, vmem, vmem),
+        out_shape=(shape, shape, shape, cache, cache),
+        in_specs=[hbm] * 9,
+        out_specs=(vmem,) * 5,
         scratch_shapes=[
+            pltpu.VMEM(hidden.shape, BF16),
+            pltpu.VMEM(gain.shape, BF16),
+            pltpu.VMEM(pos_row.shape, jnp.int32),
+            pltpu.VMEM(freq.shape, F32),
             pltpu.VMEM((width, 3 * head), BF16),
             pltpu.VMEM((side, side, CORES, rows, width), BF16),
-            pltpu.SemaphoreType.DMA((3,)),
+            pltpu.SemaphoreType.DMA((4,)),
+            pltpu.SemaphoreType.DMA((5,)),
             pltpu.SemaphoreType.DMA((GATHER_COPIES,)),
             pltpu.SemaphoreType.DMA((GATHER_COPIES,)),
         ],
-        compiler_params=pltpu.CompilerParams(collective_id=0, has_side_effects=True, vmem_limit_bytes=24 << 20),
+        compiler_params=pltpu.CompilerParams(collective_id=0, has_side_effects=True, vmem_limit_bytes=16 << 20),
         cost_estimate=pl.CostEstimate(flops=20_000_000_000, bytes_accessed=8 << 20, transcendentals=0),
         name='gather_qkv',
-    )(hidden, gain, pos_col, freq, wq, wk, wv)
+    )(*in_hbm(hidden, gain, pos_row, freq, wq, wk, wv, kc, vc))
 
 
 TOKEN_BLOCK = 16
 
 
-def attend_kernel(pos_smem, pos_ref, q_ref, k_ref, v_ref, kc_hbm, vc_hbm, o_ref, ko_hbm, vo_hbm,
-                  kbuf, vbuf, in_sem, out_sem):
+def attend_kernel(pos_smem, q_ref, k_ref, v_ref, kc_ref, vc_ref, o_ref, kbuf, vbuf, ko_hbm, vo_hbm, out_sem):
     tokens, length, head = kbuf.shape
     blocks = tokens // TOKEN_BLOCK
-    caches = ((kc_hbm, kbuf, ko_hbm), (vc_hbm, vbuf, vo_hbm))
-
-    def load(b, j):
-        src, buf, _ = caches[j]
-        at = pl.ds(b * TOKEN_BLOCK, TOKEN_BLOCK)
-        return pltpu.make_async_copy(src.at[at], buf.at[at], in_sem.at[j, b])
+    caches = ((kbuf, ko_hbm), (vbuf, vo_hbm))
 
     def store(b, j):
-        _, buf, dst = caches[j]
+        buf, dst = caches[j]
         at = pl.ds(b * TOKEN_BLOCK, TOKEN_BLOCK)
         return pltpu.make_async_copy(buf.at[at], dst.at[at], out_sem.at[j, b])
 
-    for b in range(blocks):
-        load(b, 0).start()
-        load(b, 1).start()
     group = 16
     row = lax.broadcasted_iota(jnp.int32, (group, head), 0)
     lane = lax.broadcasted_iota(jnp.int32, (TOKEN_BLOCK, length), 1)
@@ -361,11 +385,11 @@
     def block(b, carry):
         base = pl.multiple_of(b * TOKEN_BLOCK, TOKEN_BLOCK)
         at = pl.ds(base, TOKEN_BLOCK)
-        load(b, 0).wait()
-        load(b, 1).wait()
         news = (k_ref[at, :].astype(F32), v_ref[at, :].astype(F32))
+        last = jnp.zeros((TOKEN_BLOCK, length), jnp.int32)
         for t in range(TOKEN_BLOCK):
             p = pos_smem[base + t]
+            last = jnp.where(pick == t, p, last)
             lo = pl.multiple_of((p // group) * group, group)
             for j, buf in ((0, kbuf), (1, vbuf)):
                 old = buf[base + t, pl.ds(lo, group), :].astype(F32)
@@ -382,7 +406,7 @@
             lhs = jnp.concatenate([left, right], axis=1).astype(BF16)
             scores += lax.dot_general(lhs, pair, (((1,), (1,)), ((), ())), preferred_element_type=F32)
         scores = scores * (head ** -0.5)
-        scores = jnp.where(lane <= pos_ref[at, :], scores, -1e30)
+        scores = jnp.where(lane <= last, scores, -1e30)
         top = jnp.max(scores, axis=-1, keepdims=True)
         probs = jnp.exp(scores - top)
         probs = (probs / jnp.sum(probs, axis=-1, keepdims=True)).astype(BF16)
@@ -401,38 +425,39 @@
         store(b, 1).wait()
 
 
-def attend_call(positions, pos_col, q, k, v, kc, vc):
+def attend_call(positions, q, k, v, kc, vc):
     tokens, length, head = kc.shape
     blocks = tokens // TOKEN_BLOCK
-    vmem, hbm = pl.BlockSpec(memory_space=pltpu.VMEM), pl.BlockSpec(memory_space=pl.ANY)
-    cache = jax.ShapeDtypeStruct(kc.shape, BF16)
-    return pl.pallas_call(
+    vmem, hbm = pl.BlockSpec(memory_space=pltpu.VMEM), pl.BlockSpec(memory_space=pltpu.HBM)
+    cache = pltpu.VMEM(kc.shape, BF16)
+    result = pltpu.HBM(kc.shape, BF16)
+    o, _, _, ko, vo = pl.pallas_call(
         attend_kernel,
-        out_shape=(jax.ShapeDtypeStruct(q.shape, BF16), cache, cache),
-        in_specs=[pl.BlockSpec(memory_space=pltpu.SMEM), vmem, vmem, vmem, vmem, hbm, hbm],
-        out_specs=(vmem, hbm, hbm),
-        scratch_shapes=[
-            pltpu.VMEM(kc.shape, BF16),
-            pltpu.VMEM(kc.shape, BF16),
-            pltpu.SemaphoreType.DMA((2, blocks)),
-            pltpu.SemaphoreType.DMA((2, blocks)),
-        ],
-        compiler_params=pltpu.CompilerParams(vmem_limit_bytes=60 << 20),
+        out_shape=(pltpu.VMEM(q.shape, BF16), cache, cache, result, result),
+        in_specs=[pl.BlockSpec(memory_space=pltpu.SMEM)] + [vmem] * 5,
+        out_specs=(vmem, vmem, vmem, hbm, hbm),
+        input_output_aliases={4: 1, 5: 2},
+        scratch_shapes=[pltpu.SemaphoreType.DMA((2, blocks))],
+        compiler_params=pltpu.CompilerParams(vmem_limit_bytes=8 << 20),
         cost_estimate=pl.CostEstimate(flops=20_000_000_000, bytes_accessed=32 << 20, transcendentals=0),
         name='attend',
-    )(positions, pos_col, q, k, v, kc, vc)
-
-
-def block_kernel(side, x_ref, gain_ref, o_ref, wo_hbm, wg_hbm, wu_hbm, wd_hbm, out_ref,
-                 wo, wg, wu, wd, mid_rows, act, gath, w_sem, g_send, g_recv, *bufs):
+    )(positions, *in_vmem(q, k, v, kc, vc))
+    return o, ko, vo
+
+
+def block_kernel(side, x_hbm, gain_hbm, o_ref, wo_hbm, wg_hbm, wu_hbm, wd_hbm, out_ref,
+                 x_ref, gain_ref, wo, wg, wu, wd, mid_rows, act, gath, w_sem, g_send, g_recv, *bufs):
     place = Place(side)
     count = len(bufs) // 2
     loads = []
-    for i, (src, dst) in enumerate(((wo_hbm, wo), (wg_hbm, wg), (wu_hbm, wu), (wd_hbm, wd))):
+    for i, (src, dst) in enumerate(((wo_hbm, wo), (x_hbm, x_ref), (gain_hbm, gain_ref), (wg_hbm, wg), (wu_hbm, wu), (wd_hbm, wd))):
         loads.append(pltpu.make_async_copy(src, dst, w_sem.at[i]))
         loads[-1].start()
-    place.barrier()
+    place.barrier_signal()
     loads[0].wait()
+    loads[1].wait()
+    loads[2].wait()
+    place.barrier_wait()
 
     def out_proj(base, size):
         return jnp.dot(o_ref[...], wo[:, pl.ds(base, size)], preferred_element_type=F32)
@@ -444,14 +469,14 @@
     sent = reduce_scatter(place, out_proj, bufs[:count], out_done)
     gath[place.coord[0], place.coord[1], place.core] = norm_rows(mid_rows[...], gain_ref[...].astype(F32))
     sent += all_gather(place, gath, g_send, g_recv)
-    loads[1].wait()
-    loads[2].wait()
+    loads[3].wait()
+    loads[4].wait()
     rows = flat_rows(gath)
     nt = (((1,), (1,)), ((), ()))
     gate = lax.dot_general(rows, wg[...], nt, preferred_element_type=F32)
     up = lax.dot_general(rows, wu[...], nt, preferred_element_type=F32)
     act[...] = (gate * jax.nn.sigmoid(gate) * up).astype(BF16)
-    loads[3].wait()
+    loads[5].wait()
 
     def down_proj(base, size):
         return jnp.dot(act[...], wd[:, pl.ds(base, size)], preferred_element_type=F32)
@@ -468,13 +493,15 @@
 def block_call(side, hidden, gain, attn, wo, wg, wu, wd):
     rows, width = hidden.shape
     tokens = attn.shape[0]
-    vmem, hbm = pl.BlockSpec(memory_space=pltpu.VMEM), pl.BlockSpec(memory_space=pl.ANY)
+    vmem, hbm = pl.BlockSpec(memory_space=pltpu.VMEM), pl.BlockSpec(memory_space=pltpu.HBM)
     return pl.pallas_call(
         functools.partial(block_kernel, side),
         out_shape=jax.ShapeDtypeStruct(hidden.shape, BF16),
-        in_specs=[vmem, vmem, vmem, hbm, hbm, hbm, hbm],
+        in_specs=[hbm, hbm, vmem, hbm, hbm, hbm, hbm],
         out_specs=vmem,
         scratch_shapes=[
+            pltpu.VMEM(hidden.shape, BF16),
+            pltpu.VMEM(gain.shape, BF16),
             pltpu.VMEM(wo.shape, BF16),
             pltpu.VMEM(wg.shape, BF16),
             pltpu.VMEM(wu.shape, BF16),
@@ -482,14 +509,14 @@
             pltpu.VMEM((rows, width), F32),
             pltpu.VMEM((tokens, wg.shape[0]), BF16),
             pltpu.VMEM((side, side, CORES, rows, width), BF16),
-            pltpu.SemaphoreType.DMA((4,)),
+            pltpu.SemaphoreType.DMA((6,)),
             pltpu.SemaphoreType.DMA((GATHER_COPIES,)),
             pltpu.SemaphoreType.DMA((GATHER_COPIES,)),
         ] + scatter_scratch(side, rows, width) * 2,
-        compiler_params=pltpu.CompilerParams(collective_id=1, has_side_effects=True, vmem_limit_bytes=60 << 20),
+        compiler_params=pltpu.CompilerParams(collective_id=1, has_side_effects=True, vmem_limit_bytes=28 << 20),
         cost_estimate=pl.CostEstimate(flops=60_000_000_000, bytes_accessed=16 << 20, transcendentals=0),
         name='project_mlp',
-    )(hidden, gain, attn, wo, wg, wu, wd)
+    )(*in_hbm(hidden, gain), *in_vmem(attn), *in_hbm(wo, wg, wu, wd))
 
 
 def solution(mesh):
@@ -504,14 +531,15 @@
     def device_step(hidden, positions, attn_gain, mlp_gain, w_query, w_key, w_value, w_out, w_gate, w_up, w_down, k_cache, v_cache):
         n_layers, n_tokens = w_query.shape[0], positions.shape[0]
         length, heads, head = k_cache.shape[2:]
-        pos_col = positions.reshape(n_tokens, 1)
+        pos_row = positions.reshape(1, n_tokens)
         freq = ROPE_BASE ** (-2.0 * np.arange(head // 2, dtype=np.float32) / np.float32(head))
         freq = jnp.asarray(np.concatenate([freq, freq])[None, :].astype(np.float32))
         k_out, v_out = [], []
         for i in range(n_layers):
-            q, k, v = qkv_call(side, hidden, attn_gain[i:i + 1], pos_col, freq, w_query[i], w_key[i], w_value[i])
             shape = (n_tokens, length, head)
-            attn, kc, vc = attend_call(positions, pos_col, q, k, v, k_cache[i].reshape(shape), v_cache[i].reshape(shape))
+            q, k, v, kc, vc = qkv_call(side, hidden, attn_gain[i:i + 1], pos_row, freq, w_query[i], w_key[i], w_value[i],
+                                       k_cache[i].reshape(shape), v_cache[i].reshape(shape))
+            attn, kc, vc = attend_call(positions, q, k, v, kc, vc)
             k_out.append(kc.reshape(k_cache.shape[1:]))
             v_out.append(vc.reshape(v_cache.shape[1:]))
             hidden = block_call(side, hidden, mlp_gain[i:i + 1], attn, w_out[i], w_gate[i].T, w_up[i].T, w_down[i])

time: 111 us -> 96.5 us (0.87)
  local copies, waits for them, and re-layouts: 10 us -> 0.64 us
  Pallas kernels: 98.9 us -> 94 us
    unnamed x21 -> x3, local copies, waits for them, and re-layouts: 9.22 us -> 0.64 us
    pallas_call x1, Pallas kernels: 56.9 us -> 54.1 us  [block_call(): pl.pallas_call(functools.partial(block_kernel, side), out_shape=jax.Shape...]
    pallas_call x1, Pallas kernels: 16.9 us -> 14.5 us  [attend_call(): pl.pallas_call(attend_kernel, out_shape=(pltpu.VMEM(q.shape, BF16), cache...]
where the time goes in v2:
time: 96.5 us; the launch traced here: 95.3 us
  Pallas kernels  94 us (97%)
    pallas_call x1, Pallas kernels, block_call(): pl.pallas_call(functools.partial(block_kernel, side), out_shape=jax.Shape...  54.1 us
    pallas_call x1, Pallas kernels, qkv_call(): pl.pallas_call(functools.partial(qkv_kernel, side), out_shape=(shape, sha...  25.4 us
    pallas_call x1, Pallas kernels, attend_call(): pl.pallas_call(attend_kernel, out_shape=(pltpu.VMEM(q.shape, BF16), cache...  14.5 us

profile of v2, /device:TPU:97, one launch (start us, length us, event | category | flops | bytes accessed | tf_op | source)
XLA Modules:
  0.0 95.3 jit_solution(13757624173968918390)
XLA Ops:
  0.6 0.0 copy-start
  0.6 25.4 %gather_qkv.1 = (bf16[256,128]{1,0:T(8,128)(2,1)S(1)}, bf16[256,128]{1,0:T(8,128)(2,1)S(1)}, bf16[256,128]{1,0:T(8,128)(2,1)S(1)}, bf16[256,128,128]{2,1,0:T(8,128)(2,1)S(1)}, bf16[256,128,128]{2,1,0:T(8,128)(2,1)S(1)}) custom-call(bf16[8,4096]{1,0:T(8,128)(2,1)} %x_hbm.3, bf16[1,4096]{1,0:T(2,128)(2,1)} %gain_hbm.2, s32[1,256]{1,0:T(1,128)} %bitcast.20, ...), custom_call_target="tpu_custom_call" | custom-call | flops 20000000000 | bytes 8388608 | tf_op jit(solution)/shard_map/gather_qkv/pallas_call | solution.py:344
  26.0 0.0 copy-done
  26.0 14.5 %attend.1 = (bf16[256,128]{1,0:T(8,128)(2,1)S(1)}, bf16[256,128,128]{2,1,0:T(8,128)(2,1)S(1)}, bf16[256,128,128]{2,1,0:T(8,128)(2,1)S(1)}, bf16[256,128,128]{2,1,0:T(8,128)(2,1)}, bf16[256,128,128]{2,1,0:T(8,128)(2,1)}) custom-call(s32[256]{0:T(256)S(1)} %copy-done, ...), custom_call_target="tpu_custom_call", output_to_operand_aliasing={{1}: (4, {}), {2}: (5, {})} | custom-call | flops 20000000000 | bytes 33554432 | tf_op jit(solution)/shard_map/attend/pallas_call | solution.py:434
  40.6 54.1 %project_mlp.1 = bf16[8,4096]{1,0:T(8,128)(2,1)S(1)} custom-call(bf16[8,4096]{1,0:T(8,128)(2,1)} %x_hbm.3, bf16[1,4096]{1,0:T(2,128)(2,1)} %gain_hbm.3, bf16[256,128]{1,0:T(8,128)(2,1)S(1)} %get-tuple-element.16.o_ref, bf16[128,4096]{1,0:T(8,128)(2,1)} %bitcast.29, bf16[344,4096]{1,0:T(8,128)(2,1)} %bitcast.23, bf16[344,4096]{1,0:T(8,128)(2,1)} %bitcast.24, ...), custom_call_target="tpu_custom_call" | custom-call | flops 60000002048 | bytes 16777216 | tf_op jit(solution)/shard_map/project_mlp/pallas_call | solution.py:497
  94.7 0.6 copy.24
Async XLA Ops:
  0.6 25.4 %copy-start = (s32[256]{0:T(256)S(1)}, s32[256]{0:T(256)}, u32[]{:S(2)}) copy-start(s32[256]{0:T(256)} %pos_smem.1) | copy-start | bytes 3076

commit v3 on v2

v3 whole, which is shorter than its diff:
```python
import functools
import math

import jax
import jax.numpy as jnp
import numpy as np
from jax import lax
from jax.experimental import pallas as pl
from jax.experimental.pallas import tpu as pltpu
from jax.sharding import PartitionSpec as P

NORM_EPS = 1e-5
ROPE_BASE = 10000.0
CORES = 2
BF16 = jnp.bfloat16
F32 = jnp.float32


class Place:
    def __init__(self, side):
        me = lax.axis_index('model')
        self.side = side
        self.core = lax.rem(me, CORES)
        chip = me // CORES
        self.coord = (chip // side, lax.rem(chip, side))
        self.partner = self.device(self.coord, 1 - self.core)

    def device(self, coord, core):
        return {'model': (coord[0] * self.side + coord[1]) * CORES + core}

    def shift(self, axis, by):
        moved = list(self.coord)
        moved[axis] = lax.rem(moved[axis] + (by + self.side), self.side)
        return tuple(moved)

    def offset(self, first, by_first, by_second):
        moved = list(self.coord)
        moved[first] = lax.rem(moved[first] + (by_first + self.side), self.side)
        moved[1 - first] = lax.rem(moved[1 - first] + (by_second + self.side), self.side)
        return tuple(moved)

    def neighbour(self, axis, by):
        return self.device(self.shift(axis, by), self.core)

    def barrier_signal(self):
        others = [self.neighbour(axis, by) for axis in (0, 1) for by in (2, 1, -1)] + [self.partner]
        for other in others:
            pl.semaphore_signal(pltpu.get_barrier_semaphore(), inc=1, device_id=other,
                                device_id_type=pl.DeviceIdType.MESH)

    def barrier_wait(self):
        pl.semaphore_wait(pltpu.get_barrier_semaphore(), 7)


def remote(src, dst, send, recv, device):
    return pltpu.make_async_remote_copy(src_ref=src, dst_ref=dst, send_sem=send, recv_sem=recv,
                                        device_id=device, device_id_type=pl.DeviceIdType.MESH)


OFFSETS = (2, 1, -1, 0)
HALF_GATHER = 3 + 4 * 3 + 16
GATHER_COPIES = 2 * HALF_GATHER


def all_gather(place, buf, send, recv, idle=None):
    half = buf.shape[-1] // 2
    started = []

    class Half:
        def __init__(self, h):
            self.h = h
            self.first = 1 - h

        def copy(self, idx, a, b, device, core=None):
            coord = place.offset(self.first, a, b)
            ref = buf.at[coord[0], coord[1], place.core if core is None else core, :, pl.ds(self.h * half, half)]
            sem = self.h * HALF_GATHER + idx
            return remote(ref, ref, send.at[sem], recv.at[sem], device)

        def start(self, *args):
            copy = self.copy(*args)
            copy.start()
            started.append(copy)

        def first_send(self, by):
            self.start(by % 4 - 1, 0, 0, place.neighbour(self.first, by))

        def first_take(self, by):
            self.copy(by % 4 - 1, -by, 0, place.partner).wait_recv()
            self.second_send(-by)
            self.twin(-by, 0)

        def second_send(self, a):
            for by in (2, 1, -1):
                self.start(3 + 3 * (a % 4) + by % 4 - 1, a, 0, place.neighbour(1 - self.first, by))

        def second_take(self, a, by):
            self.copy(3 + 3 * (a % 4) + by % 4 - 1, a, -by, place.partner).wait_recv()
            self.twin(a, -by)

        def twin(self, a, b):
            self.start(15 + 4 * (a % 4) + b % 4, a, b, place.partner)

        def twin_take(self, a, b):
            self.copy(15 + 4 * (a % 4) + b % 4, a, b, place.partner, 1 - place.core).wait_recv()

    halves = (Half(0), Half(1))
    for by in (2, 1, -1):
        for h in halves:
            h.first_send(by)
    for h in halves:
        h.second_send(0)
        h.twin(0, 0)
    if idle is not None:
        idle()
    for by in (1, -1, 2):
        for h in halves:
            h.first_take(by)
    for a in (0, 1, -1, 2):
        for by in (1, -1, 2):
            for h in halves:
                h.second_take(a, by)
    for h in halves:
        for a in (0, 1, -1, 2):
            for b in (0, 1, -1, 2):
                h.twin_take(a, b)
    return started


HALF_SCATTER = 4 + 4 * 3 + 3
SCATTER_COPIES = 2 * HALF_SCATTER
PROJECT = 1024


def scatter_scratch(side, rows, width):
    half = width // 2
    return [
        pltpu.VMEM((side, side, CORES, rows, width), BF16),
        pltpu.VMEM((2, 4, side, rows, half), BF16),
        pltpu.VMEM((2, 4, side, rows, half), BF16),
        pltpu.VMEM((2, 4, 3, rows, half), BF16),
        pltpu.VMEM((2, 3, rows, half), BF16),
        pltpu.VMEM((2, 3, rows, half), BF16),
        pltpu.SemaphoreType.DMA((SCATTER_COPIES,)),
        pltpu.SemaphoreType.DMA((SCATTER_COPIES,)),
    ]


def reduce_scatter(place, compute, bufs, done):
    part, twin, total, land1, mid, land2, send, recv = bufs
    side, rows, width = part.shape[0], part.shape[3], part.shape[4]
    half = width // 2
    started = []

    class Half:
        def __init__(self, h):
            self.h = h
            self.first = h
            self.cols = pl.ds(h * half, half)

        def start(self, k, src, dst, device):
            sem = self.h * HALF_SCATTER + k
            copy = remote(src, dst, send.at[sem], recv.at[sem], device)
            copy.start()
            started.append(copy)

        def take(self, k, dst):
            sem = self.h * HALF_SCATTER + k
            remote(dst, dst, send.at[sem], recv.at[sem], place.partner).wait_recv()

        def group(self, j, core):
            at = place.shift(1 - self.first, j)[1 - self.first]
            return part.at[:, at, core, :, self.cols] if self.first == 0 else part.at[at, :, core, :, self.cols]

        def compute(self):
            for base in range(self.h * half, (self.h + 1) * half, PROJECT):
                value = compute(base, PROJECT).reshape(side, side, CORES, rows, PROJECT)
                part[:, :, :, :, pl.ds(base, PROJECT)] = value.astype(BF16)
            for i, j in enumerate(OFFSETS):
                self.start(i, self.group(j, 1 - place.core), twin.at[self.h, i], place.partner)

        def first_send(self, i, j):
            self.take(i, twin.at[self.h, i])
            own = self.group(j, place.core)[...].astype(F32)
            total[self.h, i] = (own + twin[self.h, i].astype(F32)).astype(BF16)
            for k, by in enumerate((2, 1, -1)):
                at = place.shift(self.first, by)[self.first]
                self.start(4 + 3 * i + k, total.at[self.h, i, at], land1.at[self.h, i, k], place.neighbour(self.first, by))

        def first_sum(self, i):
            value = total[self.h, i, place.coord[self.first]].astype(F32)
            for k in range(3):
                self.take(4 + 3 * i + k, land1.at[self.h, i, k])
                value = value + land1[self.h, i, k].astype(F32)
            return value

        def second_send(self, i, j):
            mid[self.h, i] = self.first_sum(i).astype(BF16)
            self.start(16 + i, mid.at[self.h, i], land2.at[self.h, i], place.neighbour(1 - self.first, j))

        def finish(self):
            value = self.first_sum(3)
            for i in range(3):
                self.take(16 + i, land2.at[self.h, i])
                value = value + land2[self.h, i].astype(F32)
            done(self.h * half, value)

    halves = (Half(0), Half(1))
    for h in halves:
        h.compute()
    for i, j in enumerate(OFFSETS):
        for h in halves:
            h.first_send(i, j)
    for i, j in enumerate(OFFSETS[:3]):
        for h in halves:
            h.second_send(i, j)
    for h in halves:
        h.finish()
    return started


def norm_rows(values, gain):
    inv = lax.rsqrt(jnp.mean(values * values, axis=-1, keepdims=True) + NORM_EPS)
    return (values * inv * gain).astype(BF16)


def flat_rows(buf):
    width = buf.shape[-1]
    return buf[...].astype(F32).reshape(-1, width).astype(BF16)


def qkv_kernel(side, x_hbm, gain_hbm, pos_hbm, freq_hbm, wq_hbm, wk_hbm, wv_hbm, kc_hbm, vc_hbm,
               q_ref, k_ref, v_ref, kbuf, vbuf,
               x_buf, gain_buf, pos_buf, freq_buf, w_buf, gath, s_sem, w_sem, send, recv):
    place = Place(side)
    head = q_ref.shape[1]
    small = [pltpu.make_async_copy(src, dst, s_sem.at[i]) for i, (src, dst) in enumerate(
        ((x_hbm, x_buf), (gain_hbm, gain_buf), (pos_hbm, pos_buf), (freq_hbm, freq_buf)))]
    large = [pltpu.make_async_copy(w, w_buf.at[:, pl.ds(i * head, head)], w_sem.at[i])
             for i, w in enumerate((wq_hbm, wk_hbm, wv_hbm))]
    caches = [pltpu.make_async_copy(kc_hbm, kbuf, w_sem.at[3]), pltpu.make_async_copy(vc_hbm, vbuf, w_sem.at[4])]
    for copy in small + large:
        copy.start()
    place.barrier_signal()
    for copy in small:
        copy.wait()
    own = norm_rows(x_buf[...].astype(F32), gain_buf[...].astype(F32))
    gath[place.coord[0], place.coord[1], place.core] = own
    place.barrier_wait()

    def idle():
        for copy in caches:
            copy.start()

    sent = all_gather(place, gath, send, recv, idle)
    pos = jnp.broadcast_to(pos_buf[...].astype(F32), (head, pos_buf.shape[1])).T
    angle = pos * freq_buf[...]
    cos, sin = jnp.cos(angle), jnp.sin(angle)
    lane = lax.broadcasted_iota(jnp.int32, sin.shape, 1)
    sin = jnp.where(lane < head // 2, -sin, sin)
    for copy in large:
        copy.wait()
    rows = flat_rows(gath)
    out = jnp.dot(rows, w_buf[...], preferred_element_type=F32).astype(BF16)

    def rotate(vec):
        vec = vec.astype(F32)
        return (vec * cos + pltpu.roll(vec, head // 2, 1) * sin).astype(BF16)

    q_ref[...] = rotate(out[:, :head])
    k_ref[...] = rotate(out[:, head:2 * head])
    v_ref[...] = out[:, 2 * head:]
    for copy in sent:
        copy.wait_send()
    for copy in caches:
        copy.wait()


def in_hbm(*arrays):
    return [pltpu.with_memory_space_constraint(a, pltpu.HBM) for a in arrays]


def in_vmem(*arrays):
    return [pltpu.with_memory_space_constraint(a, pltpu.VMEM) for a in arrays]


def qkv_call(side, hidden, gain, pos_row, freq, wq, wk, wv, kc, vc):
    rows, width = hidden.shape
    tokens = pos_row.shape[1]
    head = wq.shape[1]
    vmem, hbm = pl.BlockSpec(memory_space=pltpu.VMEM), pl.BlockSpec(memory_space=pltpu.HBM)
    shape = pltpu.VMEM((tokens, head), BF16)
    cache = pltpu.VMEM(kc.shape, BF16)
    return pl.pallas_call(
        functools.partial(qkv_kernel, side),
        out_shape=(shape, shape, shape, cache, cache),
        in_specs=[hbm] * 9,
        out_specs=(vmem,) * 5,
        scratch_shapes=[
            pltpu.VMEM(hidden.shape, BF16),
            pltpu.VMEM(gain.shape, BF16),
            pltpu.VMEM(pos_row.shape, jnp.int32),
            pltpu.VMEM(freq.shape, F32),
            pltpu.VMEM((width, 3 * head), BF16),
            pltpu.VMEM((side, side, CORES, rows, width), BF16),
            pltpu.SemaphoreType.DMA((4,)),
            pltpu.SemaphoreType.DMA((5,)),
            pltpu.SemaphoreType.DMA((GATHER_COPIES,)),
            pltpu.SemaphoreType.DMA((GATHER_COPIES,)),
        ],
        compiler_params=pltpu.CompilerParams(collective_id=0, has_side_effects=True, vmem_limit_bytes=16 << 20),
        cost_estimate=pl.CostEstimate(flops=20_000_000_000, bytes_accessed=8 << 20, transcendentals=0),
        name='gather_qkv',
    )(*in_hbm(hidden, gain, pos_row, freq, wq, wk, wv, kc, vc))


TOKEN_BLOCK = 16
SPAN = 64


def attend_kernel(pos_smem, q_ref, k_ref, v_ref, kc_ref, vc_ref, o_ref, kbuf, vbuf, ko_hbm, vo_hbm, s_buf, out_sem):
    tokens, length, head = kbuf.shape
    spans = tokens // SPAN
    caches = ((kbuf, k_ref, ko_hbm), (vbuf, v_ref, vo_hbm))
    group = 16
    row = lax.broadcasted_iota(jnp.int32, (group, head), 0)
    lane = lax.broadcasted_iota(jnp.int32, (TOKEN_BLOCK, length), 1)
    pick = lax.broadcasted_iota(jnp.int32, (TOKEN_BLOCK, head), 0)

    def store(i, j):
        buf, _, dst = caches[j]
        at = pl.ds(i * SPAN, SPAN)
        return pltpu.make_async_copy(buf.at[at], dst.at[at], out_sem.at[j, i])

    def insert(i, j):
        buf, new_ref, _ = caches[j]
        for b in range(0, SPAN, TOKEN_BLOCK):
            base = pl.multiple_of(i * SPAN + b, TOKEN_BLOCK)
            news = new_ref[pl.ds(base, TOKEN_BLOCK), :].astype(F32)
            for t in range(TOKEN_BLOCK):
                p = pos_smem[base + t]
                lo = pl.multiple_of((p // group) * group, group)
                old = buf[base + t, pl.ds(lo, group), :]
                new = jnp.broadcast_to(news[t:t + 1, :], (group, head)).astype(BF16)
                buf[base + t, pl.ds(lo, group), :] = jnp.where(row == p - lo, new, old)

    def score(i, carry):
        insert(i, 0)
        store(i, 0).start()
        insert(i, 1)
        store(i, 1).start()
        for b in range(0, SPAN, TOKEN_BLOCK):
            base = pl.multiple_of(i * SPAN + b, TOKEN_BLOCK)
            q = q_ref[pl.ds(base, TOKEN_BLOCK), :].astype(F32)
            scores = jnp.zeros((TOKEN_BLOCK, length), F32)
            last = jnp.zeros((TOKEN_BLOCK, length), jnp.int32)
            for t in range(0, TOKEN_BLOCK, 2):
                pair = jnp.concatenate([kbuf[base + t], kbuf[base + t + 1]], axis=1)
                left = jnp.where(pick == t, q, 0.0)
                right = jnp.where(pick == t + 1, q, 0.0)
                lhs = jnp.concatenate([left, right], axis=1).astype(BF16)
                scores += lax.dot_general(lhs, pair, (((1,), (1,)), ((), ())), preferred_element_type=F32)
            for t in range(TOKEN_BLOCK):
                last = jnp.where(pick == t, pos_smem[base + t], last)
            s_buf[pl.ds(base, TOKEN_BLOCK), :] = jnp.where(lane <= last, scores * (head ** -0.5), -1e30)
        return carry

    def mix(i, carry):
        for b in range(0, SPAN, TOKEN_BLOCK):
            base = pl.multiple_of(i * SPAN + b, TOKEN_BLOCK)
            probs = s_buf[pl.ds(base, TOKEN_BLOCK), :].astype(BF16)
            mixed = jnp.zeros((TOKEN_BLOCK, head), F32)
            for t in range(0, TOKEN_BLOCK, 2):
                pair = jnp.concatenate([vbuf[base + t], vbuf[base + t + 1]], axis=1)
                both = jnp.dot(probs, pair, preferred_element_type=F32)
                mixed = jnp.where(pick == t, both[:, :head], mixed)
                mixed = jnp.where(pick == t + 1, both[:, head:], mixed)
            o_ref[pl.ds(base, TOKEN_BLOCK), :] = mixed.astype(BF16)
        return carry

    lax.fori_loop(0, spans, score, 0)
    scores = s_buf[...]
    probs = jnp.exp(scores - jnp.max(scores, axis=-1, keepdims=True))
    s_buf[...] = probs / jnp.sum(probs, axis=-1, keepdims=True)
    lax.fori_loop(0, spans, mix, 0)
    for i in range(spans):
        store(i, 0).wait()
        store(i, 1).wait()


def attend_call(positions, q, k, v, kc, vc):
    tokens, length, head = kc.shape
    vmem, hbm = pl.BlockSpec(memory_space=pltpu.VMEM), pl.BlockSpec(memory_space=pltpu.HBM)
    cache = pltpu.VMEM(kc.shape, BF16)
    result = pltpu.HBM(kc.shape, BF16)
    o, _, _, ko, vo = pl.pallas_call(
        attend_kernel,
        out_shape=(pltpu.VMEM(q.shape, BF16), cache, cache, result, result),
        in_specs=[pl.BlockSpec(memory_space=pltpu.SMEM)] + [vmem] * 5,
        out_specs=(vmem, vmem, vmem, hbm, hbm),
        input_output_aliases={4: 1, 5: 2},
        scratch_shapes=[pltpu.VMEM((tokens, length), F32), pltpu.SemaphoreType.DMA((2, tokens // SPAN))],
        compiler_params=pltpu.CompilerParams(vmem_limit_bytes=8 << 20),
        cost_estimate=pl.CostEstimate(flops=20_000_000_000, bytes_accessed=32 << 20, transcendentals=0),
        name='attend',
    )(positions, *in_vmem(q, k, v, kc, vc))
    return o, ko, vo


def block_kernel(side, x_hbm, gain_hbm, o_ref, wo_hbm, wg_hbm, wu_hbm, wd_hbm, out_ref,
                 x_ref, gain_ref, wo, wg, wu, wd, mid_rows, act, gath, w_sem, g_send, g_recv, *bufs):
    place = Place(side)
    count = len(bufs) // 2
    loads = []
    for i, (src, dst) in enumerate(((wo_hbm, wo), (x_hbm, x_ref), (gain_hbm, gain_ref), (wg_hbm, wg), (wu_hbm, wu), (wd_hbm, wd))):
        loads.append(pltpu.make_async_copy(src, dst, w_sem.at[i]))
        loads[-1].start()
    place.barrier_signal()
    loads[0].wait()
    loads[1].wait()
    loads[2].wait()
    place.barrier_wait()

    def out_proj(base, size):
        return jnp.dot(o_ref[...], wo[:, pl.ds(base, size)], preferred_element_type=F32)

    def out_done(base, value):
        cols = pl.ds(base, value.shape[1])
        mid_rows[:, cols] = (x_ref[:, cols].astype(F32) + value).astype(BF16).astype(F32)

    sent = reduce_scatter(place, out_proj, bufs[:count], out_done)
    gath[place.coord[0], place.coord[1], place.core] = norm_rows(mid_rows[...], gain_ref[...].astype(F32))
    sent += all_gather(place, gath, g_send, g_recv)
    loads[3].wait()
    loads[4].wait()
    rows = flat_rows(gath)
    nt = (((1,), (1,)), ((), ()))
    gate = lax.dot_general(rows, wg[...], nt, preferred_element_type=F32)
    up = lax.dot_general(rows, wu[...], nt, preferred_element_type=F32)
    act[...] = (gate * jax.nn.sigmoid(gate) * up).astype(BF16)
    loads[5].wait()

    def down_proj(base, size):
        return jnp.dot(act[...], wd[:, pl.ds(base, size)], preferred_element_type=F32)

    def down_done(base, value):
        cols = pl.ds(base, value.shape[1])
        out_ref[:, cols] = (mid_rows[:, cols] + value).astype(BF16)

    sent += reduce_scatter(place, down_proj, bufs[count:], down_done)
    for copy in sent:
        copy.wait_send()


def block_call(side, hidden, gain, attn, wo, wg, wu, wd):
    rows, width = hidden.shape
    tokens = attn.shape[0]
    vmem, hbm = pl.BlockSpec(memory_space=pltpu.VMEM), pl.BlockSpec(memory_space=pltpu.HBM)
    return pl.pallas_call(
        functools.partial(block_kernel, side),
        out_shape=jax.ShapeDtypeStruct(hidden.shape, BF16),
        in_specs=[hbm, hbm, vmem, hbm, hbm, hbm, hbm],
        out_specs=vmem,
        scratch_shapes=[
            pltpu.VMEM(hidden.shape, BF16),
            pltpu.VMEM(gain.shape, BF16),
            pltpu.VMEM(wo.shape, BF16),
            pltpu.VMEM(wg.shape, BF16),
            pltpu.VMEM(wu.shape, BF16),
            pltpu.VMEM(wd.shape, BF16),
            pltpu.VMEM((rows, width), F32),
            pltpu.VMEM((tokens, wg.shape[0]), BF16),
            pltpu.VMEM((side, side, CORES, rows, width), BF16),
            pltpu.SemaphoreType.DMA((6,)),
            pltpu.SemaphoreType.DMA((GATHER_COPIES,)),
            pltpu.SemaphoreType.DMA((GATHER_COPIES,)),
        ] + scatter_scratch(side, rows, width) * 2,
        compiler_params=pltpu.CompilerParams(collective_id=1, has_side_effects=True, vmem_limit_bytes=28 << 20),
        cost_estimate=pl.CostEstimate(flops=60_000_000_000, bytes_accessed=16 << 20, transcendentals=0),
        name='project_mlp',
    )(*in_hbm(hidden, gain), *in_vmem(attn), *in_hbm(wo, wg, wu, wd))


def solution(mesh):
    row_spec = P(('data', 'model'), None)
    cache_spec = P(None, 'data', None, 'model', None)
    col_spec = P(None, None, 'model')
    inner_spec = P(None, 'model', None)
    in_specs = (row_spec, P('data'), P(), P(), col_spec, col_spec, col_spec, inner_spec, col_spec, col_spec, inner_spec, cache_spec, cache_spec)
    out_specs = (row_spec, cache_spec, cache_spec)
    side = math.isqrt(mesh.shape['model'] // CORES)

    def device_step(hidden, positions, attn_gain, mlp_gain, w_query, w_key, w_value, w_out, w_gate, w_up, w_down, k_cache, v_cache):
        n_layers, n_tokens = w_query.shape[0], positions.shape[0]
        length, heads, head = k_cache.shape[2:]
        pos_row = positions.reshape(1, n_tokens)
        freq = ROPE_BASE ** (-2.0 * np.arange(head // 2, dtype=np.float32) / np.float32(head))
        freq = jnp.asarray(np.concatenate([freq, freq])[None, :].astype(np.float32))
        k_out, v_out = [], []
        for i in range(n_layers):
            shape = (n_tokens, length, head)
            q, k, v, kc, vc = qkv_call(side, hidden, attn_gain[i:i + 1], pos_row, freq, w_query[i], w_key[i], w_value[i],
                                       k_cache[i].reshape(shape), v_cache[i].reshape(shape))
            attn, kc, vc = attend_call(positions, q, k, v, kc, vc)
            k_out.append(kc.reshape(k_cache.shape[1:]))
            v_out.append(vc.reshape(v_cache.shape[1:]))
            hidden = block_call(side, hidden, mlp_gain[i:i + 1], attn, w_out[i], w_gate[i].T, w_up[i].T, w_down[i])
        return hidden, jnp.stack(k_out), jnp.stack(v_out)

    return jax.shard_map(device_step, mesh=mesh, in_specs=in_specs, out_specs=out_specs, check_vma=False)
```

time: 96.5 us -> 72.5 us (0.75); the launches traced: 95.3 us -> 72.4 us
  Pallas kernels: 94 us -> 71.1 us
    pallas_call x1, Pallas kernels: 54.1 us -> 41.7 us  [block_call(): pl.pallas_call(functools.partial(block_kernel, side), out_shape=jax.Shape...]
    pallas_call x1, Pallas kernels: 14.5 us -> 7.49 us  [attend_call(): pl.pallas_call(attend_kernel, out_shape=(pltpu.VMEM(q.shape, BF16), cache...]
    pallas_call x1, Pallas kernels: 25.4 us -> 21.9 us  [qkv_call(): pl.pallas_call(functools.partial(qkv_kernel, side), out_shape=(shape, sha...]
where the time goes in v3:
time: 72.5 us; the launch traced here: 72.4 us
  Pallas kernels  71.1 us (98%)
    pallas_call x1, Pallas kernels, block_call(): pl.pallas_call(functools.partial(block_kernel, side), out_shape=jax.Shape...  41.7 us
    pallas_call x1, Pallas kernels, qkv_call(): pl.pallas_call(functools.partial(qkv_kernel, side), out_shape=(shape, sha...  21.9 us
    pallas_call x1, Pallas kernels, attend_call(): pl.pallas_call(attend_kernel, out_shape=(pltpu.VMEM(q.shape, BF16), cache...  7.49 us

profile of v3, /device:TPU:97, one launch (start us, length us, event | category | flops | bytes accessed | tf_op | source)
XLA Modules:
  0.0 72.4 jit_solution(4643251116497829790)
XLA Ops:
  0.6 0.0 copy-start
  0.6 21.9 %gather_qkv.1 = (bf16[256,128]{1,0:T(8,128)(2,1)S(1)}, bf16[256,128]{1,0:T(8,128)(2,1)S(1)}, bf16[256,128]{1,0:T(8,128)(2,1)S(1)}, bf16[256,128,128]{2,1,0:T(8,128)(2,1)S(1)}, bf16[256,128,128]{2,1,0:T(8,128)(2,1)S(1)}) custom-call(bf16[8,4096]{1,0:T(8,128)(2,1)} %x_hbm.3, bf16[1,4096]{1,0:T(2,128)(2,1)} %gain_hbm.2, s32[1,256]{1,0:T(1,128)} %bitcast.20, ...), custom_call_target="tpu_custom_call" | custom-call | flops 20000000000 | bytes 8388608 | tf_op jit(solution)/shard_map/gather_qkv/pallas_call | solution.py:294
  22.5 0.0 copy-done
  22.5 7.5 %attend.1 = (bf16[256,128]{1,0:T(8,128)(2,1)S(1)}, bf16[256,128,128]{2,1,0:T(8,128)(2,1)S(1)}, bf16[256,128,128]{2,1,0:T(8,128)(2,1)S(1)}, bf16[256,128,128]{2,1,0:T(8,128)(2,1)}, bf16[256,128,128]{2,1,0:T(8,128)(2,1)}) custom-call(s32[256]{0:T(256)S(1)} %copy-done, ...), custom_call_target="tpu_custom_call", output_to_operand_aliasing={{1}: (4, {}), {2}: (5, {})} | custom-call | flops 20000000000 | bytes 33554432 | tf_op jit(solution)/shard_map/attend/pallas_call | solution.py:396
  30.0 41.7 %project_mlp.1 = bf16[8,4096]{1,0:T(8,128)(2,1)S(1)} custom-call(bf16[8,4096]{1,0:T(8,128)(2,1)} %x_hbm.3, bf16[1,4096]{1,0:T(2,128)(2,1)} %gain_hbm.3, bf16[256,128]{1,0:T(8,128)(2,1)S(1)} %get-tuple-element.16.o_ref, bf16[128,4096]{1,0:T(8,128)(2,1)} %bitcast.29, bf16[344,4096]{1,0:T(8,128)(2,1)} %bitcast.23, bf16[344,4096]{1,0:T(8,128)(2,1)} %bitcast.24, ...), custom_call_target="tpu_custom_call" | custom-call | flops 60000002048 | bytes 16777216 | tf_op jit(solution)/shard_map/project_mlp/pallas_call | solution.py:459
  71.8 0.6 copy.24
Async XLA Ops:
  0.6 21.9 %copy-start = (s32[256]{0:T(256)S(1)}, s32[256]{0:T(256)}, u32[]{:S(2)}) copy-start(s32[256]{0:T(256)} %pos_smem.1) | copy-start | bytes 3076

commit v4 on v3

--- a/solution.py
+++ b/solution.py
@@ -42,14 +42,19 @@
     def neighbour(self, axis, by):
         return self.device(self.shift(axis, by), self.core)
 
-    def barrier_signal(self):
+    def diagonal(self, by):
+        return self.device(self.offset(0, by, by), self.core)
+
+    def barrier_signal(self, diagonal=True):
         others = [self.neighbour(axis, by) for axis in (0, 1) for by in (2, 1, -1)] + [self.partner]
+        if diagonal:
+            others += [self.diagonal(by) for by in (1, -1)]
         for other in others:
             pl.semaphore_signal(pltpu.get_barrier_semaphore(), inc=1, device_id=other,
                                 device_id_type=pl.DeviceIdType.MESH)
 
-    def barrier_wait(self):
-        pl.semaphore_wait(pltpu.get_barrier_semaphore(), 7)
+    def barrier_wait(self, diagonal=True):
+        pl.semaphore_wait(pltpu.get_barrier_semaphore(), 9 if diagonal else 7)
 
 
 def remote(src, dst, send, recv, device):
@@ -62,7 +67,7 @@
 GATHER_COPIES = 2 * HALF_GATHER
 
 
-def all_gather(place, buf, send, recv, idle=None):
+def all_gather(place, buf, send, recv, idle=None, diagonal=True):
     half = buf.shape[-1] // 2
     started = []
 
@@ -92,7 +97,12 @@
 
         def second_send(self, a):
             for by in (2, 1, -1):
-                self.start(3 + 3 * (a % 4) + by % 4 - 1, a, 0, place.neighbour(1 - self.first, by))
+                if not diagonal or abs(by) == 2 or a + by != 0:
+                    self.start(3 + 3 * (a % 4) + by % 4 - 1, a, 0, place.neighbour(1 - self.first, by))
+
+        def diagonal_send(self):
+            for by in (1, -1):
+                self.start(3 + 3 * (-by % 4) + by % 4 - 1, 0, 0, place.diagonal(by))
 
         def second_take(self, a, by):
             self.copy(3 + 3 * (a % 4) + by % 4 - 1, a, -by, place.partner).wait_recv()
@@ -110,6 +120,8 @@
             h.first_send(by)
     for h in halves:
         h.second_send(0)
+        if diagonal:
+            h.diagonal_send()
         h.twin(0, 0)
     if idle is not None:
         idle()
@@ -231,7 +243,7 @@
 
 def qkv_kernel(side, x_hbm, gain_hbm, pos_hbm, freq_hbm, wq_hbm, wk_hbm, wv_hbm, kc_hbm, vc_hbm,
                q_ref, k_ref, v_ref, kbuf, vbuf,
-               x_buf, gain_buf, pos_buf, freq_buf, w_buf, gath, s_sem, w_sem, send, recv):
+               x_buf, gain_buf, pos_buf, freq_buf, rope, w_buf, gath, s_sem, w_sem, send, recv):
     place = Place(side)
     head = q_ref.shape[1]
     small = [pltpu.make_async_copy(src, dst, s_sem.at[i]) for i, (src, dst) in enumerate(
@@ -241,23 +253,24 @@
     caches = [pltpu.make_async_copy(kc_hbm, kbuf, w_sem.at[3]), pltpu.make_async_copy(vc_hbm, vbuf, w_sem.at[4])]
     for copy in small + large:
         copy.start()
-    place.barrier_signal()
+    place.barrier_signal(diagonal=False)
     for copy in small:
         copy.wait()
     own = norm_rows(x_buf[...].astype(F32), gain_buf[...].astype(F32))
     gath[place.coord[0], place.coord[1], place.core] = own
-    place.barrier_wait()
+    place.barrier_wait(diagonal=False)
 
     def idle():
         for copy in caches:
             copy.start()
-
-    sent = all_gather(place, gath, send, recv, idle)
-    pos = jnp.broadcast_to(pos_buf[...].astype(F32), (head, pos_buf.shape[1])).T
-    angle = pos * freq_buf[...]
-    cos, sin = jnp.cos(angle), jnp.sin(angle)
-    lane = lax.broadcasted_iota(jnp.int32, sin.shape, 1)
-    sin = jnp.where(lane < head // 2, -sin, sin)
+        pos = jnp.broadcast_to(pos_buf[...].astype(F32), (head, pos_buf.shape[1])).T
+        angle = pos * freq_buf[...]
+        sin = jnp.sin(angle)
+        lane = lax.broadcasted_iota(jnp.int32, sin.shape, 1)
+        rope[0] = jnp.cos(angle)
+        rope[1] = jnp.where(lane < head // 2, -sin, sin)
+
+    sent = all_gather(place, gath, send, recv, idle, diagonal=False)
     for copy in large:
         copy.wait()
     rows = flat_rows(gath)
@@ -265,7 +278,7 @@
 
     def rotate(vec):
         vec = vec.astype(F32)
-        return (vec * cos + pltpu.roll(vec, head // 2, 1) * sin).astype(BF16)
+        return (vec * rope[0] + pltpu.roll(vec, head // 2, 1) * rope[1]).astype(BF16)
 
     q_ref[...] = rotate(out[:, :head])
     k_ref[...] = rotate(out[:, head:2 * head])
@@ -301,6 +314,7 @@
             pltpu.VMEM(gain.shape, BF16),
             pltpu.VMEM(pos_row.shape, jnp.int32),
             pltpu.VMEM(freq.shape, F32),
+            pltpu.VMEM((2, tokens, head), F32),
             pltpu.VMEM((width, 3 * head), BF16),
             pltpu.VMEM((side, side, CORES, rows, width), BF16),
             pltpu.SemaphoreType.DMA((4,)),

time: 72.5 us -> 73.1 us (level)
    pallas_call x1, Pallas kernels: 41.7 us -> 42.9 us  [block_call(): pl.pallas_call(functools.partial(block_kernel, side), out_shape=jax.Shape...]
where the time goes in v4:
time: 73.1 us; the launch traced here: 73 us
  Pallas kernels  71.7 us (98%)
    pallas_call x1, Pallas kernels, block_call(): pl.pallas_call(functools.partial(block_kernel, side), out_shape=jax.Shape...  42.9 us
    pallas_call x1, Pallas kernels, qkv_call(): pl.pallas_call(functools.partial(qkv_kernel, side), out_shape=(shape, sha...  21.3 us
    pallas_call x1, Pallas kernels, attend_call(): pl.pallas_call(attend_kernel, out_shape=(pltpu.VMEM(q.shape, BF16), cache...  7.49 us

profile of v4, /device:TPU:97, one launch (start us, length us, event | category | flops | bytes accessed | tf_op | source)
XLA Modules:
  0.0 73.0 jit_solution(18237378563729847453)
XLA Ops:
  0.6 0.0 copy-start
  0.6 21.3 %gather_qkv.1 = (bf16[256,128]{1,0:T(8,128)(2,1)S(1)}, bf16[256,128]{1,0:T(8,128)(2,1)S(1)}, bf16[256,128]{1,0:T(8,128)(2,1)S(1)}, bf16[256,128,128]{2,1,0:T(8,128)(2,1)S(1)}, bf16[256,128,128]{2,1,0:T(8,128)(2,1)S(1)}) custom-call(bf16[8,4096]{1,0:T(8,128)(2,1)} %x_hbm.3, bf16[1,4096]{1,0:T(2,128)(2,1)} %gain_hbm.2, s32[1,256]{1,0:T(1,128)} %bitcast.20, ...), custom_call_target="tpu_custom_call" | custom-call | flops 20000000000 | bytes 8388608 | tf_op jit(solution)/shard_map/gather_qkv/pallas_call | solution.py:307
  22.0 0.0 copy-done
  22.0 7.5 %attend.1 = (bf16[256,128]{1,0:T(8,128)(2,1)S(1)}, bf16[256,128,128]{2,1,0:T(8,128)(2,1)S(1)}, bf16[256,128,128]{2,1,0:T(8,128)(2,1)S(1)}, bf16[256,128,128]{2,1,0:T(8,128)(2,1)}, bf16[256,128,128]{2,1,0:T(8,128)(2,1)}) custom-call(s32[256]{0:T(256)S(1)} %copy-done, ...), custom_call_target="tpu_custom_call", output_to_operand_aliasing={{1}: (4, {}), {2}: (5, {})} | custom-call | flops 20000000000 | bytes 33554432 | tf_op jit(solution)/shard_map/attend/pallas_call | solution.py:410
  29.5 42.9 %project_mlp.1 = bf16[8,4096]{1,0:T(8,128)(2,1)S(1)} custom-call(bf16[8,4096]{1,0:T(8,128)(2,1)} %x_hbm.3, bf16[1,4096]{1,0:T(2,128)(2,1)} %gain_hbm.3, bf16[256,128]{1,0:T(8,128)(2,1)S(1)} %get-tuple-element.16.o_ref, bf16[128,4096]{1,0:T(8,128)(2,1)} %bitcast.29, bf16[344,4096]{1,0:T(8,128)(2,1)} %bitcast.23, bf16[344,4096]{1,0:T(8,128)(2,1)} %bitcast.24, ...), custom_call_target="tpu_custom_call" | custom-call | flops 60000002048 | bytes 16777216 | tf_op jit(solution)/shard_map/project_mlp/pallas_call | solution.py:473
  72.4 0.6 copy.24
Async XLA Ops:
  0.6 21.3 %copy-start = (s32[256]{0:T(256)S(1)}, s32[256]{0:T(256)}, u32[]{:S(2)}) copy-start(s32[256]{0:T(256)} %pos_smem.1) | copy-start | bytes 3076

commit v5 on v3

--- a/solution.py
+++ b/solution.py
@@ -146,7 +146,7 @@
     ]
 
 
-def reduce_scatter(place, compute, bufs, done):
+def reduce_scatter(place, compute, bufs, done, ready=None):
     part, twin, total, land1, mid, land2, send, recv = bufs
     side, rows, width = part.shape[0], part.shape[3], part.shape[4]
     half = width // 2
@@ -172,10 +172,12 @@
             at = place.shift(1 - self.first, j)[1 - self.first]
             return part.at[:, at, core, :, self.cols] if self.first == 0 else part.at[at, :, core, :, self.cols]
 
-        def compute(self):
+        def project(self):
             for base in range(self.h * half, (self.h + 1) * half, PROJECT):
                 value = compute(base, PROJECT).reshape(side, side, CORES, rows, PROJECT)
                 part[:, :, :, :, pl.ds(base, PROJECT)] = value.astype(BF16)
+
+        def twins(self):
             for i, j in enumerate(OFFSETS):
                 self.start(i, self.group(j, 1 - place.core), twin.at[self.h, i], place.partner)
 
@@ -207,7 +209,10 @@
 
     halves = (Half(0), Half(1))
     for h in halves:
-        h.compute()
+        h.project()
+        if h.h == 0 and ready is not None:
+            ready()
+        h.twins()
     for i, j in enumerate(OFFSETS):
         for h in halves:
             h.first_send(i, j)
@@ -231,7 +236,7 @@
 
 def qkv_kernel(side, x_hbm, gain_hbm, pos_hbm, freq_hbm, wq_hbm, wk_hbm, wv_hbm, kc_hbm, vc_hbm,
                q_ref, k_ref, v_ref, kbuf, vbuf,
-               x_buf, gain_buf, pos_buf, freq_buf, w_buf, gath, s_sem, w_sem, send, recv):
+               x_buf, gain_buf, pos_buf, freq_buf, rope, w_buf, gath, s_sem, w_sem, send, recv):
     place = Place(side)
     head = q_ref.shape[1]
     small = [pltpu.make_async_copy(src, dst, s_sem.at[i]) for i, (src, dst) in enumerate(
@@ -251,13 +256,14 @@
     def idle():
         for copy in caches:
             copy.start()
+        pos = jnp.broadcast_to(pos_buf[...].astype(F32), (head, pos_buf.shape[1])).T
+        angle = pos * freq_buf[...]
+        sin = jnp.sin(angle)
+        lane = lax.broadcasted_iota(jnp.int32, sin.shape, 1)
+        rope[0] = jnp.cos(angle)
+        rope[1] = jnp.where(lane < head // 2, -sin, sin)
 
     sent = all_gather(place, gath, send, recv, idle)
-    pos = jnp.broadcast_to(pos_buf[...].astype(F32), (head, pos_buf.shape[1])).T
-    angle = pos * freq_buf[...]
-    cos, sin = jnp.cos(angle), jnp.sin(angle)
-    lane = lax.broadcasted_iota(jnp.int32, sin.shape, 1)
-    sin = jnp.where(lane < head // 2, -sin, sin)
     for copy in large:
         copy.wait()
     rows = flat_rows(gath)
@@ -265,7 +271,7 @@
 
     def rotate(vec):
         vec = vec.astype(F32)
-        return (vec * cos + pltpu.roll(vec, head // 2, 1) * sin).astype(BF16)
+        return (vec * rope[0] + pltpu.roll(vec, head // 2, 1) * rope[1]).astype(BF16)
 
     q_ref[...] = rotate(out[:, :head])
     k_ref[...] = rotate(out[:, head:2 * head])
@@ -301,6 +307,7 @@
             pltpu.VMEM(gain.shape, BF16),
             pltpu.VMEM(pos_row.shape, jnp.int32),
             pltpu.VMEM(freq.shape, F32),
+            pltpu.VMEM((2, tokens, head), F32),
             pltpu.VMEM((width, 3 * head), BF16),
             pltpu.VMEM((side, side, CORES, rows, width), BF16),
             pltpu.SemaphoreType.DMA((4,)),
@@ -316,6 +323,7 @@
 
 TOKEN_BLOCK = 16
 SPAN = 64
+STORE = 32
 
 
 def attend_kernel(pos_smem, q_ref, k_ref, v_ref, kc_ref, vc_ref, o_ref, kbuf, vbuf, ko_hbm, vo_hbm, s_buf, out_sem):
@@ -329,28 +337,28 @@
 
     def store(i, j):
         buf, _, dst = caches[j]
-        at = pl.ds(i * SPAN, SPAN)
+        at = pl.ds(i * STORE, STORE)
         return pltpu.make_async_copy(buf.at[at], dst.at[at], out_sem.at[j, i])
 
-    def insert(i, j):
+    def insert(base, j):
         buf, new_ref, _ = caches[j]
+        news = new_ref[pl.ds(base, TOKEN_BLOCK), :].astype(F32)
+        for t in range(TOKEN_BLOCK):
+            p = pos_smem[base + t]
+            lo = pl.multiple_of((p // group) * group, group)
+            old = buf[base + t, pl.ds(lo, group), :]
+            new = jnp.broadcast_to(news[t:t + 1, :], (group, head)).astype(BF16)
+            buf[base + t, pl.ds(lo, group), :] = jnp.where(row == p - lo, new, old)
+
+    def score(i, carry):
         for b in range(0, SPAN, TOKEN_BLOCK):
             base = pl.multiple_of(i * SPAN + b, TOKEN_BLOCK)
-            news = new_ref[pl.ds(base, TOKEN_BLOCK), :].astype(F32)
-            for t in range(TOKEN_BLOCK):
-                p = pos_smem[base + t]
-                lo = pl.multiple_of((p // group) * group, group)
-                old = buf[base + t, pl.ds(lo, group), :]
-                new = jnp.broadcast_to(news[t:t + 1, :], (group, head)).astype(BF16)
-                buf[base + t, pl.ds(lo, group), :] = jnp.where(row == p - lo, new, old)
-
-    def score(i, carry):
-        insert(i, 0)
-        store(i, 0).start()
-        insert(i, 1)
-        store(i, 1).start()
-        for b in range(0, SPAN, TOKEN_BLOCK):
-            base = pl.multiple_of(i * SPAN + b, TOKEN_BLOCK)
+            insert(base, 0)
+            insert(base, 1)
+            if (b + TOKEN_BLOCK) % STORE == 0:
+                at = i * (SPAN // STORE) + b // STORE
+                store(at, 0).start()
+                store(at, 1).start()
             q = q_ref[pl.ds(base, TOKEN_BLOCK), :].astype(F32)
             scores = jnp.zeros((TOKEN_BLOCK, length), F32)
             last = jnp.zeros((TOKEN_BLOCK, length), jnp.int32)
@@ -383,7 +391,7 @@
     probs = jnp.exp(scores - jnp.max(scores, axis=-1, keepdims=True))
     s_buf[...] = probs / jnp.sum(probs, axis=-1, keepdims=True)
     lax.fori_loop(0, spans, mix, 0)
-    for i in range(spans):
+    for i in range(tokens // STORE):
         store(i, 0).wait()
         store(i, 1).wait()
 
@@ -399,7 +407,7 @@
         in_specs=[pl.BlockSpec(memory_space=pltpu.SMEM)] + [vmem] * 5,
         out_specs=(vmem, vmem, vmem, hbm, hbm),
         input_output_aliases={4: 1, 5: 2},
-        scratch_shapes=[pltpu.VMEM((tokens, length), F32), pltpu.SemaphoreType.DMA((2, tokens // SPAN))],
+        scratch_shapes=[pltpu.VMEM((tokens, length), F32), pltpu.SemaphoreType.DMA((2, tokens // STORE))],
         compiler_params=pltpu.CompilerParams(vmem_limit_bytes=8 << 20),
         cost_estimate=pl.CostEstimate(flops=20_000_000_000, bytes_accessed=32 << 20, transcendentals=0),
         name='attend',
@@ -419,7 +427,6 @@
     loads[0].wait()
     loads[1].wait()
     loads[2].wait()
-    place.barrier_wait()
 
     def out_proj(base, size):
         return jnp.dot(o_ref[...], wo[:, pl.ds(base, size)], preferred_element_type=F32)
@@ -428,7 +435,7 @@
         cols = pl.ds(base, value.shape[1])
         mid_rows[:, cols] = (x_ref[:, cols].astype(F32) + value).astype(BF16).astype(F32)
 
-    sent = reduce_scatter(place, out_proj, bufs[:count], out_done)
+    sent = reduce_scatter(place, out_proj, bufs[:count], out_done, place.barrier_wait)
     gath[place.coord[0], place.coord[1], place.core] = norm_rows(mid_rows[...], gain_ref[...].astype(F32))
     sent += all_gather(place, gath, g_send, g_recv)
     loads[3].wait()

time: 72.5 us -> 71.1 us (0.981)
  Pallas kernels: 71.1 us -> 69.8 us
where the time goes in v5:
time: 71.1 us
  Pallas kernels  69.8 us (98%)
    pallas_call x1, Pallas kernels, block_call(): pl.pallas_call(functools.partial(block_kernel, side), out_shape=jax.Shape...  41.4 us
    pallas_call x1, Pallas kernels, qkv_call(): pl.pallas_call(functools.partial(qkv_kernel, side), out_shape=(shape, sha...  21.3 us
    pallas_call x1, Pallas kernels, attend_call(): pl.pallas_call(attend_kernel, out_shape=(pltpu.VMEM(q.shape, BF16), cache...  7.09 us

profile of v5, /device:TPU:97, one launch (start us, length us, event | category | flops | bytes accessed | tf_op | source)
XLA Modules:
  0.0 71.1 jit_solution(8992730726030124823)
XLA Ops:
  0.6 0.0 copy-start
  0.6 21.3 %gather_qkv.1 = (bf16[256,128]{1,0:T(8,128)(2,1)S(1)}, bf16[256,128]{1,0:T(8,128)(2,1)S(1)}, bf16[256,128]{1,0:T(8,128)(2,1)S(1)}, bf16[256,128,128]{2,1,0:T(8,128)(2,1)S(1)}, bf16[256,128,128]{2,1,0:T(8,128)(2,1)S(1)}) custom-call(bf16[8,4096]{1,0:T(8,128)(2,1)} %x_hbm.3, bf16[1,4096]{1,0:T(2,128)(2,1)} %gain_hbm.2, s32[1,256]{1,0:T(1,128)} %bitcast.20, ...), custom_call_target="tpu_custom_call" | custom-call | flops 20000000000 | bytes 8388608 | tf_op jit(solution)/shard_map/gather_qkv/pallas_call | solution.py:300
  22.0 0.0 copy-done
  22.0 7.1 %attend.1 = (bf16[256,128]{1,0:T(8,128)(2,1)S(1)}, bf16[256,128,128]{2,1,0:T(8,128)(2,1)S(1)}, bf16[256,128,128]{2,1,0:T(8,128)(2,1)S(1)}, bf16[256,128,128]{2,1,0:T(8,128)(2,1)}, bf16[256,128,128]{2,1,0:T(8,128)(2,1)}) custom-call(s32[256]{0:T(256)S(1)} %copy-done, ...), custom_call_target="tpu_custom_call", output_to_operand_aliasing={{1}: (4, {}), {2}: (5, {})} | custom-call | flops 20000000000 | bytes 33554432 | tf_op jit(solution)/shard_map/attend/pallas_call | solution.py:404
  29.1 41.4 %project_mlp.1 = bf16[8,4096]{1,0:T(8,128)(2,1)S(1)} custom-call(bf16[8,4096]{1,0:T(8,128)(2,1)} %x_hbm.3, bf16[1,4096]{1,0:T(2,128)(2,1)} %gain_hbm.3, bf16[256,128]{1,0:T(8,128)(2,1)S(1)} %get-tuple-element.16.o_ref, bf16[128,4096]{1,0:T(8,128)(2,1)} %bitcast.29, bf16[344,4096]{1,0:T(8,128)(2,1)} %bitcast.23, bf16[344,4096]{1,0:T(8,128)(2,1)} %bitcast.24, ...), custom_call_target="tpu_custom_call" | custom-call | flops 60000002048 | bytes 16777216 | tf_op jit(solution)/shard_map/project_mlp/pallas_call | solution.py:466
  70.5 0.6 copy.24
Async XLA Ops:
  0.6 21.3 %copy-start = (s32[256]{0:T(256)S(1)}, s32[256]{0:T(256)}, u32[]{:S(2)}) copy-start(s32[256]{0:T(256)} %pos_smem.1) | copy-start | bytes 3076

commit v6 on v5

--- a/solution.py
+++ b/solution.py
@@ -58,32 +58,39 @@
 
 
 OFFSETS = (2, 1, -1, 0)
-HALF_GATHER = 3 + 4 * 3 + 16
-GATHER_COPIES = 2 * HALF_GATHER
+HALF_GATHER = 3 + 4 * 3
+GATHER_WAITS = 2 * HALF_GATHER + 1
+
+
+def all_sent(buf, sem):
+    side, _, cores, rows, width = buf.shape
+    total = (side * side * cores - 1) * rows * width
+
+    def wait(ref):
+        count, rest = divmod(total, math.prod(ref.shape[1:]))
+        assert rest == 0 and count <= ref.shape[0]
+        span = ref.at[pl.ds(0, count)]
+        pltpu.make_async_copy(span, span, sem).wait()
+
+    return wait
 
 
 def all_gather(place, buf, send, recv, idle=None):
     half = buf.shape[-1] // 2
-    started = []
 
     class Half:
         def __init__(self, h):
             self.h = h
             self.first = 1 - h
 
-        def copy(self, idx, a, b, device, core=None):
+        def copy(self, idx, a, b, device):
             coord = place.offset(self.first, a, b)
-            ref = buf.at[coord[0], coord[1], place.core if core is None else core, :, pl.ds(self.h * half, half)]
-            sem = self.h * HALF_GATHER + idx
-            return remote(ref, ref, send.at[sem], recv.at[sem], device)
-
-        def start(self, *args):
-            copy = self.copy(*args)
-            copy.start()
-            started.append(copy)
+            ref = buf.at[coord[0], coord[1], place.core, :, pl.ds(self.h * half, half)]
+            sem = 2 * HALF_GATHER if idx is None else self.h * HALF_GATHER + idx
+            return remote(ref, ref, send.at[0], recv.at[sem], device)
 
         def first_send(self, by):
-            self.start(by % 4 - 1, 0, 0, place.neighbour(self.first, by))
+            self.copy(by % 4 - 1, 0, 0, place.neighbour(self.first, by)).start()
 
         def first_take(self, by):
             self.copy(by % 4 - 1, -by, 0, place.partner).wait_recv()
@@ -92,17 +99,14 @@
 
         def second_send(self, a):
             for by in (2, 1, -1):
-                self.start(3 + 3 * (a % 4) + by % 4 - 1, a, 0, place.neighbour(1 - self.first, by))
+                self.copy(3 + 3 * (a % 4) + by % 4 - 1, a, 0, place.neighbour(1 - self.first, by)).start()
 
         def second_take(self, a, by):
             self.copy(3 + 3 * (a % 4) + by % 4 - 1, a, -by, place.partner).wait_recv()
             self.twin(a, -by)
 
         def twin(self, a, b):
-            self.start(15 + 4 * (a % 4) + b % 4, a, b, place.partner)
-
-        def twin_take(self, a, b):
-            self.copy(15 + 4 * (a % 4) + b % 4, a, b, place.partner, 1 - place.core).wait_recv()
+            self.copy(None, a, b, place.partner).start()
 
     halves = (Half(0), Half(1))
     for by in (2, 1, -1):
@@ -120,15 +124,13 @@
         for by in (1, -1, 2):
             for h in halves:
                 h.second_take(a, by)
-    for h in halves:
-        for a in (0, 1, -1, 2):
-            for b in (0, 1, -1, 2):
-                h.twin_take(a, b)
-    return started
-
-
-HALF_SCATTER = 4 + 4 * 3 + 3
-SCATTER_COPIES = 2 * HALF_SCATTER
+    theirs = buf.at[:, :, 1 - place.core]
+    remote(theirs, theirs, send.at[0], recv.at[2 * HALF_GATHER], place.partner).wait_recv()
+    return all_sent(buf, send.at[0])
+
+
+HALF_SCATTER = 4 + 4 + 1
+SCATTER_WAITS = 2 * HALF_SCATTER
 PROJECT = 1024
 
 
@@ -141,8 +143,8 @@
         pltpu.VMEM((2, 4, 3, rows, half), BF16),
         pltpu.VMEM((2, 3, rows, half), BF16),
         pltpu.VMEM((2, 3, rows, half), BF16),
-        pltpu.SemaphoreType.DMA((SCATTER_COPIES,)),
-        pltpu.SemaphoreType.DMA((SCATTER_COPIES,)),
+        pltpu.SemaphoreType.DMA((1,)),
+        pltpu.SemaphoreType.DMA((SCATTER_WAITS,)),
     ]
 
 
@@ -150,7 +152,6 @@
     part, twin, total, land1, mid, land2, send, recv = bufs
     side, rows, width = part.shape[0], part.shape[3], part.shape[4]
     half = width // 2
-    started = []
 
     class Half:
         def __init__(self, h):
@@ -160,13 +161,11 @@
 
         def start(self, k, src, dst, device):
             sem = self.h * HALF_SCATTER + k
-            copy = remote(src, dst, send.at[sem], recv.at[sem], device)
-            copy.start()
-            started.append(copy)
+            remote(src, dst, send.at[0], recv.at[sem], device).start()
 
         def take(self, k, dst):
             sem = self.h * HALF_SCATTER + k
-            remote(dst, dst, send.at[sem], recv.at[sem], place.partner).wait_recv()
+            remote(dst, dst, send.at[0], recv.at[sem], place.partner).wait_recv()
 
         def group(self, j, core):
             at = place.shift(1 - self.first, j)[1 - self.first]
@@ -187,23 +186,23 @@
             total[self.h, i] = (own + twin[self.h, i].astype(F32)).astype(BF16)
             for k, by in enumerate((2, 1, -1)):
                 at = place.shift(self.first, by)[self.first]
-                self.start(4 + 3 * i + k, total.at[self.h, i, at], land1.at[self.h, i, k], place.neighbour(self.first, by))
+                self.start(4 + i, total.at[self.h, i, at], land1.at[self.h, i, k], place.neighbour(self.first, by))
 
         def first_sum(self, i):
             value = total[self.h, i, place.coord[self.first]].astype(F32)
+            self.take(4 + i, land1.at[self.h, i])
             for k in range(3):
-                self.take(4 + 3 * i + k, land1.at[self.h, i, k])
                 value = value + land1[self.h, i, k].astype(F32)
             return value
 
         def second_send(self, i, j):
             mid[self.h, i] = self.first_sum(i).astype(BF16)
-            self.start(16 + i, mid.at[self.h, i], land2.at[self.h, i], place.neighbour(1 - self.first, j))
+            self.start(8, mid.at[self.h, i], land2.at[self.h, i], place.neighbour(1 - self.first, j))
 
         def finish(self):
             value = self.first_sum(3)
+            self.take(8, land2.at[self.h])
             for i in range(3):
-                self.take(16 + i, land2.at[self.h, i])
                 value = value + land2[self.h, i].astype(F32)
             done(self.h * half, value)
 
@@ -221,7 +220,7 @@
             h.second_send(i, j)
     for h in halves:
         h.finish()
-    return started
+    return all_sent(part, send.at[0])
 
 
 def norm_rows(values, gain):
@@ -276,10 +275,9 @@
     q_ref[...] = rotate(out[:, :head])
     k_ref[...] = rotate(out[:, head:2 * head])
     v_ref[...] = out[:, 2 * head:]
-    for copy in sent:
-        copy.wait_send()
     for copy in caches:
         copy.wait()
+    sent(kbuf)
 
 
 def in_hbm(*arrays):
@@ -312,8 +310,8 @@
             pltpu.VMEM((side, side, CORES, rows, width), BF16),
             pltpu.SemaphoreType.DMA((4,)),
             pltpu.SemaphoreType.DMA((5,)),
-            pltpu.SemaphoreType.DMA((GATHER_COPIES,)),
-            pltpu.SemaphoreType.DMA((GATHER_COPIES,)),
+            pltpu.SemaphoreType.DMA((1,)),
+            pltpu.SemaphoreType.DMA((GATHER_WAITS,)),
         ],
         compiler_params=pltpu.CompilerParams(collective_id=0, has_side_effects=True, vmem_limit_bytes=16 << 20),
         cost_estimate=pl.CostEstimate(flops=20_000_000_000, bytes_accessed=8 << 20, transcendentals=0),
@@ -435,9 +433,9 @@
         cols = pl.ds(base, value.shape[1])
         mid_rows[:, cols] = (x_ref[:, cols].astype(F32) + value).astype(BF16).astype(F32)
 
-    sent = reduce_scatter(place, out_proj, bufs[:count], out_done, place.barrier_wait)
+    sent = [reduce_scatter(place, out_proj, bufs[:count], out_done, place.barrier_wait)]
     gath[place.coord[0], place.coord[1], place.core] = norm_rows(mid_rows[...], gain_ref[...].astype(F32))
-    sent += all_gather(place, gath, g_send, g_recv)
+    sent.append(all_gather(place, gath, g_send, g_recv))
     loads[3].wait()
     loads[4].wait()
     rows = flat_rows(gath)
@@ -454,9 +452,9 @@
         cols = pl.ds(base, value.shape[1])
         out_ref[:, cols] = (mid_rows[:, cols] + value).astype(BF16)
 
-    sent += reduce_scatter(place, down_proj, bufs[count:], down_done)
-    for copy in sent:
-        copy.wait_send()
+    sent.append(reduce_scatter(place, down_proj, bufs[count:], down_done))
+    for wait in sent:
+        wait(wd)
 
 
 def block_call(side, hidden, gain, attn, wo, wg, wu, wd):
@@ -479,8 +477,8 @@
             pltpu.VMEM((tokens, wg.shape[0]), BF16),
             pltpu.VMEM((side, side, CORES, rows, width), BF16),
             pltpu.SemaphoreType.DMA((6,)),
-            pltpu.SemaphoreType.DMA((GATHER_COPIES,)),
-            pltpu.SemaphoreType.DMA((GATHER_COPIES,)),
+            pltpu.SemaphoreType.DMA((1,)),
+            pltpu.SemaphoreType.DMA((GATHER_WAITS,)),
         ] + scatter_scratch(side, rows, width) * 2,
         compiler_params=pltpu.CompilerParams(collective_id=1, has_side_effects=True, vmem_limit_bytes=28 << 20),
         cost_estimate=pl.CostEstimate(flops=60_000_000_000, bytes_accessed=16 << 20, transcendentals=0),

time: 71.1 us -> 68.1 us (0.958)
  Pallas kernels: 69.8 us -> 66.7 us
    pallas_call x1, Pallas kernels: 41.4 us -> 39.2 us  [block_call(): pl.pallas_call(functools.partial(block_kernel, side), out_shape=jax.Shape...]
    pallas_call x1, Pallas kernels: 21.3 us -> 20.4 us  [qkv_call(): pl.pallas_call(functools.partial(qkv_kernel, side), out_shape=(shape, sha...]
where the time goes in v6:
time: 68.1 us; the launch traced here: 68 us
  Pallas kernels  66.7 us (98%)
    pallas_call x1, Pallas kernels, block_call(): pl.pallas_call(functools.partial(block_kernel, side), out_shape=jax.Shape...  39.2 us
    pallas_call x1, Pallas kernels, qkv_call(): pl.pallas_call(functools.partial(qkv_kernel, side), out_shape=(shape, sha...  20.4 us
    pallas_call x1, Pallas kernels, attend_call(): pl.pallas_call(attend_kernel, out_shape=(pltpu.VMEM(q.shape, BF16), cache...  7.08 us

profile of v6, /device:TPU:97, one launch (start us, length us, event | category | flops | bytes accessed | tf_op | source)
XLA Modules:
  0.0 68.0 jit_solution(15597681062889067051)
XLA Ops:
  0.6 0.0 copy-start
  0.6 20.4 %gather_qkv.1 = (bf16[256,128]{1,0:T(8,128)(2,1)S(1)}, bf16[256,128]{1,0:T(8,128)(2,1)S(1)}, bf16[256,128]{1,0:T(8,128)(2,1)S(1)}, bf16[256,128,128]{2,1,0:T(8,128)(2,1)S(1)}, bf16[256,128,128]{2,1,0:T(8,128)(2,1)S(1)}) custom-call(bf16[8,4096]{1,0:T(8,128)(2,1)} %x_hbm.3, bf16[1,4096]{1,0:T(2,128)(2,1)} %gain_hbm.2, s32[1,256]{1,0:T(1,128)} %bitcast.20, ...), custom_call_target="tpu_custom_call" | custom-call | flops 20000000000 | bytes 8388608 | tf_op jit(solution)/shard_map/gather_qkv/pallas_call | solution.py:298
  21.1 0.0 copy-done
  21.1 7.1 %attend.1 = (bf16[256,128]{1,0:T(8,128)(2,1)S(1)}, bf16[256,128,128]{2,1,0:T(8,128)(2,1)S(1)}, bf16[256,128,128]{2,1,0:T(8,128)(2,1)S(1)}, bf16[256,128,128]{2,1,0:T(8,128)(2,1)}, bf16[256,128,128]{2,1,0:T(8,128)(2,1)}) custom-call(s32[256]{0:T(256)S(1)} %copy-done, ...), custom_call_target="tpu_custom_call", output_to_operand_aliasing={{1}: (4, {}), {2}: (5, {})} | custom-call | flops 20000000000 | bytes 33554432 | tf_op jit(solution)/shard_map/attend/pallas_call | solution.py:402
  28.2 39.2 %project_mlp.1 = bf16[8,4096]{1,0:T(8,128)(2,1)S(1)} custom-call(bf16[8,4096]{1,0:T(8,128)(2,1)} %x_hbm.3, bf16[1,4096]{1,0:T(2,128)(2,1)} %gain_hbm.3, bf16[256,128]{1,0:T(8,128)(2,1)S(1)} %get-tuple-element.16.o_ref, bf16[128,4096]{1,0:T(8,128)(2,1)} %bitcast.29, bf16[344,4096]{1,0:T(8,128)(2,1)} %bitcast.23, bf16[344,4096]{1,0:T(8,128)(2,1)} %bitcast.24, ...), custom_call_target="tpu_custom_call" | custom-call | flops 60000002048 | bytes 16777216 | tf_op jit(solution)/shard_map/project_mlp/pallas_call | solution.py:464
  67.4 0.6 copy.24
Async XLA Ops:
  0.6 20.4 %copy-start = (s32[256]{0:T(256)S(1)}, s32[256]{0:T(256)}, u32[]{:S(2)}) copy-start(s32[256]{0:T(256)} %pos_smem.1) | copy-start | bytes 3076

commit v7 on v6

--- a/solution.py
+++ b/solution.py
@@ -58,7 +58,7 @@
 
 
 OFFSETS = (2, 1, -1, 0)
-HALF_GATHER = 3 + 4 * 3
+HALF_GATHER = 3 + 4
 GATHER_WAITS = 2 * HALF_GATHER + 1
 
 
@@ -86,8 +86,7 @@
         def copy(self, idx, a, b, device):
             coord = place.offset(self.first, a, b)
             ref = buf.at[coord[0], coord[1], place.core, :, pl.ds(self.h * half, half)]
-            sem = 2 * HALF_GATHER if idx is None else self.h * HALF_GATHER + idx
-            return remote(ref, ref, send.at[0], recv.at[sem], device)
+            return remote(ref, ref, send.at[0], recv.at[self.h * HALF_GATHER + idx], device)
 
         def first_send(self, by):
             self.copy(by % 4 - 1, 0, 0, place.neighbour(self.first, by)).start()
@@ -95,18 +94,21 @@
         def first_take(self, by):
             self.copy(by % 4 - 1, -by, 0, place.partner).wait_recv()
             self.second_send(-by)
-            self.twin(-by, 0)
 
         def second_send(self, a):
             for by in (2, 1, -1):
-                self.copy(3 + 3 * (a % 4) + by % 4 - 1, a, 0, place.neighbour(1 - self.first, by)).start()
-
-        def second_take(self, a, by):
-            self.copy(3 + 3 * (a % 4) + by % 4 - 1, a, -by, place.partner).wait_recv()
-            self.twin(a, -by)
-
-        def twin(self, a, b):
-            self.copy(None, a, b, place.partner).start()
+                self.copy(3 + a % 4, a, 0, place.neighbour(1 - self.first, by)).start()
+
+        def line(self, a, count):
+            at = place.offset(self.first, a, 0)[self.first]
+            cols = pl.ds(self.h * half, half)
+            span = pl.ds(0, count)
+            return buf.at[span, at, place.core, :, cols] if self.first else buf.at[at, span, place.core, :, cols]
+
+        def second_take(self, a):
+            got, line = self.line(a, 3), self.line(a, 4)
+            remote(got, got, send.at[0], recv.at[self.h * HALF_GATHER + 3 + a % 4], place.partner).wait_recv()
+            remote(line, line, send.at[0], recv.at[2 * HALF_GATHER], place.partner).start()
 
     halves = (Half(0), Half(1))
     for by in (2, 1, -1):
@@ -114,16 +116,14 @@
             h.first_send(by)
     for h in halves:
         h.second_send(0)
-        h.twin(0, 0)
     if idle is not None:
         idle()
     for by in (1, -1, 2):
         for h in halves:
             h.first_take(by)
-    for a in (0, 1, -1, 2):
-        for by in (1, -1, 2):
-            for h in halves:
-                h.second_take(a, by)
+    for a in (0, -1, 1, 2):
+        for h in halves:
+            h.second_take(a)
     theirs = buf.at[:, :, 1 - place.core]
     remote(theirs, theirs, send.at[0], recv.at[2 * HALF_GATHER], place.partner).wait_recv()
     return all_sent(buf, send.at[0])
@@ -351,12 +351,11 @@
     def score(i, carry):
         for b in range(0, SPAN, TOKEN_BLOCK):
             base = pl.multiple_of(i * SPAN + b, TOKEN_BLOCK)
-            insert(base, 0)
-            insert(base, 1)
-            if (b + TOKEN_BLOCK) % STORE == 0:
-                at = i * (SPAN // STORE) + b // STORE
-                store(at, 0).start()
-                store(at, 1).start()
+            if b % STORE == 0:
+                for j in (0, 1):
+                    for more in range(0, STORE, TOKEN_BLOCK):
+                        insert(pl.multiple_of(base + more, TOKEN_BLOCK), j)
+                    store(i * (SPAN // STORE) + b // STORE, j).start()
             q = q_ref[pl.ds(base, TOKEN_BLOCK), :].astype(F32)
             scores = jnp.zeros((TOKEN_BLOCK, length), F32)
             last = jnp.zeros((TOKEN_BLOCK, length), jnp.int32)

time: 68.1 us -> 67.9 us (level)
  no operation moved by 1% of the time
where the time goes in v7:
time: 67.9 us; the launch traced here: 67.8 us
  Pallas kernels  66.5 us (98%)
    pallas_call x1, Pallas kernels, block_call(): pl.pallas_call(functools.partial(block_kernel, side), out_shape=jax.Shape...  39.3 us
    pallas_call x1, Pallas kernels, qkv_call(): pl.pallas_call(functools.partial(qkv_kernel, side), out_shape=(shape, sha...  20.2 us
    pallas_call x1, Pallas kernels, attend_call(): pl.pallas_call(attend_kernel, out_shape=(pltpu.VMEM(q.shape, BF16), cache...  6.99 us

profile of v7, /device:TPU:97, one launch (start us, length us, event | category | flops | bytes accessed | tf_op | source)
XLA Modules:
  0.0 67.8 jit_solution(3412663360030517231)
XLA Ops:
  0.6 0.0 copy-start
  0.6 20.2 %gather_qkv.1 = (bf16[256,128]{1,0:T(8,128)(2,1)S(1)}, bf16[256,128]{1,0:T(8,128)(2,1)S(1)}, bf16[256,128]{1,0:T(8,128)(2,1)S(1)}, bf16[256,128,128]{2,1,0:T(8,128)(2,1)S(1)}, bf16[256,128,128]{2,1,0:T(8,128)(2,1)S(1)}) custom-call(bf16[8,4096]{1,0:T(8,128)(2,1)} %x_hbm.3, bf16[1,4096]{1,0:T(2,128)(2,1)} %gain_hbm.2, s32[1,256]{1,0:T(1,128)} %bitcast.20, ...), custom_call_target="tpu_custom_call" | custom-call | flops 20000000000 | bytes 8388608 | tf_op jit(solution)/shard_map/gather_qkv/pallas_call | solution.py:298
  20.9 0.0 copy-done
  20.9 7.0 %attend.1 = (bf16[256,128]{1,0:T(8,128)(2,1)S(1)}, bf16[256,128,128]{2,1,0:T(8,128)(2,1)S(1)}, bf16[256,128,128]{2,1,0:T(8,128)(2,1)S(1)}, bf16[256,128,128]{2,1,0:T(8,128)(2,1)}, bf16[256,128,128]{2,1,0:T(8,128)(2,1)}) custom-call(s32[256]{0:T(256)S(1)} %copy-done, ...), custom_call_target="tpu_custom_call", output_to_operand_aliasing={{1}: (4, {}), {2}: (5, {})} | custom-call | flops 20000000000 | bytes 33554432 | tf_op jit(solution)/shard_map/attend/pallas_call | solution.py:401
  27.9 39.3 %project_mlp.1 = bf16[8,4096]{1,0:T(8,128)(2,1)S(1)} custom-call(bf16[8,4096]{1,0:T(8,128)(2,1)} %x_hbm.3, bf16[1,4096]{1,0:T(2,128)(2,1)} %gain_hbm.3, bf16[256,128]{1,0:T(8,128)(2,1)S(1)} %get-tuple-element.16.o_ref, bf16[128,4096]{1,0:T(8,128)(2,1)} %bitcast.29, bf16[344,4096]{1,0:T(8,128)(2,1)} %bitcast.23, bf16[344,4096]{1,0:T(8,128)(2,1)} %bitcast.24, ...), custom_call_target="tpu_custom_call" | custom-call | flops 60000002048 | bytes 16777216 | tf_op jit(solution)/shard_map/project_mlp/pallas_call | solution.py:463
  67.2 0.6 copy.24
Async XLA Ops:
  0.6 20.2 %copy-start = (s32[256]{0:T(256)S(1)}, s32[256]{0:T(256)}, u32[]{:S(2)}) copy-start(s32[256]{0:T(256)} %pos_smem.1) | copy-start | bytes 3076

commit v8 on v7

--- a/solution.py
+++ b/solution.py
@@ -180,11 +180,15 @@
             for i, j in enumerate(OFFSETS):
                 self.start(i, self.group(j, 1 - place.core), twin.at[self.h, i], place.partner)
 
-        def first_send(self, i, j):
+        def merge(self, i, j):
             self.take(i, twin.at[self.h, i])
             own = self.group(j, place.core)[...].astype(F32)
             total[self.h, i] = (own + twin[self.h, i].astype(F32)).astype(BF16)
+
+        def first_send(self, i, *moves):
             for k, by in enumerate((2, 1, -1)):
+                if by not in moves:
+                    continue
                 at = place.shift(self.first, by)[self.first]
                 self.start(4 + i, total.at[self.h, i, at], land1.at[self.h, i, k], place.neighbour(self.first, by))
 
@@ -212,10 +216,20 @@
         if h.h == 0 and ready is not None:
             ready()
         h.twins()
-    for i, j in enumerate(OFFSETS):
+    for i, j in enumerate(OFFSETS[:3]):
         for h in halves:
-            h.first_send(i, j)
-    for i, j in enumerate(OFFSETS[:3]):
+            h.merge(i, j)
+            h.first_send(i, 2, 1, -1)
+    for h in halves:
+        h.merge(3, 0)
+        h.first_send(3, 2)
+    for h in halves:
+        h.first_send(3, 1)
+    for h in halves:
+        h.second_send(0, 2)
+    for h in halves:
+        h.first_send(3, -1)
+    for i, j in ((1, 1), (2, -1)):
         for h in halves:
             h.second_send(i, j)
     for h in halves:
@@ -243,11 +257,13 @@
     large = [pltpu.make_async_copy(w, w_buf.at[:, pl.ds(i * head, head)], w_sem.at[i])
              for i, w in enumerate((wq_hbm, wk_hbm, wv_hbm))]
     caches = [pltpu.make_async_copy(kc_hbm, kbuf, w_sem.at[3]), pltpu.make_async_copy(vc_hbm, vbuf, w_sem.at[4])]
-    for copy in small + large:
+    small[0].start()
+    small[1].start()
+    place.barrier_signal()
+    for copy in small[2:] + large:
         copy.start()
-    place.barrier_signal()
-    for copy in small:
-        copy.wait()
+    small[0].wait()
+    small[1].wait()
     own = norm_rows(x_buf[...].astype(F32), gain_buf[...].astype(F32))
     gath[place.coord[0], place.coord[1], place.core] = own
     place.barrier_wait()
@@ -255,6 +271,8 @@
     def idle():
         for copy in caches:
             copy.start()
+        small[2].wait()
+        small[3].wait()
         pos = jnp.broadcast_to(pos_buf[...].astype(F32), (head, pos_buf.shape[1])).T
         angle = pos * freq_buf[...]
         sin = jnp.sin(angle)
@@ -420,10 +438,14 @@
     for i, (src, dst) in enumerate(((wo_hbm, wo), (x_hbm, x_ref), (gain_hbm, gain_ref), (wg_hbm, wg), (wu_hbm, wu), (wd_hbm, wd))):
         loads.append(pltpu.make_async_copy(src, dst, w_sem.at[i]))
         loads[-1].start()
-    place.barrier_signal()
+        if i == 0:
+            place.barrier_signal()
     loads[0].wait()
-    loads[1].wait()
-    loads[2].wait()
+
+    def ready():
+        place.barrier_wait()
+        loads[1].wait()
+        loads[2].wait()
 
     def out_proj(base, size):
         return jnp.dot(o_ref[...], wo[:, pl.ds(base, size)], preferred_element_type=F32)
@@ -432,7 +454,7 @@
         cols = pl.ds(base, value.shape[1])
         mid_rows[:, cols] = (x_ref[:, cols].astype(F32) + value).astype(BF16).astype(F32)
 
-    sent = [reduce_scatter(place, out_proj, bufs[:count], out_done, place.barrier_wait)]
+    sent = [reduce_scatter(place, out_proj, bufs[:count], out_done, ready)]
     gath[place.coord[0], place.coord[1], place.core] = norm_rows(mid_rows[...], gain_ref[...].astype(F32))
     sent.append(all_gather(place, gath, g_send, g_recv))
     loads[3].wait()

time: 67.9 us -> 66.8 us (0.984)
  Pallas kernels: 66.5 us -> 65.2 us
    pallas_call x1, Pallas kernels: 20.2 us -> 19.5 us  [qkv_call(): pl.pallas_call(functools.partial(qkv_kernel, side), out_shape=(shape, sha...]
where the time goes in v8:
time: 66.8 us; the launch traced here: 66.6 us
  Pallas kernels  65.2 us (98%)
  between operations  0.67 us (1%)
    pallas_call x1, Pallas kernels, block_call(): pl.pallas_call(functools.partial(block_kernel, side), out_shape=jax.Shape...  38.7 us
    pallas_call x1, Pallas kernels, qkv_call(): pl.pallas_call(functools.partial(qkv_kernel, side), out_shape=(shape, sha...  19.5 us
    pallas_call x1, Pallas kernels, attend_call(): pl.pallas_call(attend_kernel, out_shape=(pltpu.VMEM(q.shape, BF16), cache...  6.99 us

profile of v8, /device:TPU:97, one launch (start us, length us, event | category | flops | bytes accessed | tf_op | source)
XLA Modules:
  0.0 66.6 jit_solution(12728703069943477670)
XLA Ops:
  0.6 0.0 copy-start
  0.6 19.5 %gather_qkv.1 = (bf16[256,128]{1,0:T(8,128)(2,1)S(1)}, bf16[256,128]{1,0:T(8,128)(2,1)S(1)}, bf16[256,128]{1,0:T(8,128)(2,1)S(1)}, bf16[256,128,128]{2,1,0:T(8,128)(2,1)S(1)}, bf16[256,128,128]{2,1,0:T(8,128)(2,1)S(1)}) custom-call(bf16[8,4096]{1,0:T(8,128)(2,1)} %x_hbm.3, bf16[1,4096]{1,0:T(2,128)(2,1)} %gain_hbm.2, s32[1,256]{1,0:T(1,128)} %bitcast.20, ...), custom_call_target="tpu_custom_call" | custom-call | flops 20000000000 | bytes 8388608 | tf_op jit(solution)/shard_map/gather_qkv/pallas_call | solution.py:316
  20.2 0.0 copy-done
  20.2 7.0 %attend.1 = (bf16[256,128]{1,0:T(8,128)(2,1)S(1)}, bf16[256,128,128]{2,1,0:T(8,128)(2,1)S(1)}, bf16[256,128,128]{2,1,0:T(8,128)(2,1)S(1)}, bf16[256,128,128]{2,1,0:T(8,128)(2,1)}, bf16[256,128,128]{2,1,0:T(8,128)(2,1)}) custom-call(s32[256]{0:T(256)S(1)} %copy-done, ...), custom_call_target="tpu_custom_call", output_to_operand_aliasing={{1}: (4, {}), {2}: (5, {})} | custom-call | flops 20000000000 | bytes 33554432 | tf_op jit(solution)/shard_map/attend/pallas_call | solution.py:419
  27.2 38.7 %project_mlp.1 = bf16[8,4096]{1,0:T(8,128)(2,1)S(1)} custom-call(bf16[8,4096]{1,0:T(8,128)(2,1)} %x_hbm.3, bf16[1,4096]{1,0:T(2,128)(2,1)} %gain_hbm.3, bf16[256,128]{1,0:T(8,128)(2,1)S(1)} %get-tuple-element.16.o_ref, bf16[128,4096]{1,0:T(8,128)(2,1)} %bitcast.29, bf16[344,4096]{1,0:T(8,128)(2,1)} %bitcast.23, bf16[344,4096]{1,0:T(8,128)(2,1)} %bitcast.24, ...), custom_call_target="tpu_custom_call" | custom-call | flops 60000002048 | bytes 16777216 | tf_op jit(solution)/shard_map/project_mlp/pallas_call | solution.py:485
  65.9 0.6 copy.24
Async XLA Ops:
  0.6 19.5 %copy-start = (s32[256]{0:T(256)S(1)}, s32[256]{0:T(256)}, u32[]{:S(2)}) copy-start(s32[256]{0:T(256)} %pos_smem.1) | copy-start | bytes 3076
